TPU v7x, 32 devices: a whole 2x2x4 slice. The times are simulated.
32 devices in a mesh: blk: 8 (over y, x, core), grp: 4 (over z).
Axes of the slice: x: 2, y: 2, z: 4, core: 2. Of those that a mesh axis runs over, the one named last changes fastest.
Arguments:
- image_embeds: bfloat16 [4096, 1152], P(('blk', 'grp')), may hold values from -6 to 6
- text_embeds: bfloat16 [4096, 1152], P(('blk', 'grp')), may hold values from -6 to 6
Outputs:
- image_embed_gradient: bfloat16 [4096, 1152], P(('blk', 'grp'))
- text_embed_gradient: bfloat16 [4096, 1152], P(('blk', 'grp'))
All inputs are finite; a program needn't handle non-finite values.
Results may differ from a plain program's by a relative error of at most 0.0059.
Values may be sent and summed in bfloat16 or wider, within the bound.
A program may use at most 64 MiB of HBM per device.

v0:
```python
import functools

import jax
import jax.numpy as jnp
from jax import lax
from jax.experimental import pallas as pl
from jax.experimental.pallas import tpu as pltpu
from jax.sharding import PartitionSpec as P

LOGIT_SCALE = 10.0
BIAS_LOGIT = -2.0
EPSILON = 1e-06
MESH = pl.DeviceIdType.MESH


def kernel(chips, depth, reach, window, image_ref, text_ref, image_out, text_out,
           held, total, own_scale, local_sem, send_sem, recv_sem):
    blk = lax.axis_index("blk")
    grp = lax.axis_index("grp")
    chip, core = blk // 2, blk % 2
    relayed = chips == 4 and reach == 2 and 4 * depth - 1 < window

    def view(kind):
        return (
            chip + kind * (chips - 1 - 2 * chip),
            core + kind * (1 - 2 * core),
            grp + kind * (depth - 1 - 2 * grp),
        )

    def device(kind, c, k, z):
        c = (c + chips) % chips
        linear = 2 * c + k
        return (
            linear + kind * (2 * chips - 1 - 2 * linear),
            z + kind * (depth - 1 - 2 * z),
        )

    first_kind = 1 - chip % 2 if relayed else 0
    kinds = (first_kind, 1 - first_kind)

    def need(k, z, d, source_k, source_z):
        offset = (2 * d + k - source_k) * depth + z - source_z
        return (offset >= 0) & (offset < window)

    def chip_need(z, d, source_k, source_z):
        return need(0, z, d, source_k, source_z) | need(1, z, d, source_k, source_z)

    def arrives(kind, d, source_z):
        c, k, z = view(kind)
        wanted = chip_need(z, d, k, source_z)
        if relayed:
            wanted = wanted | ((d == 2) & (c % 2 == 1))
        return wanted

    def copy(kind, path, source_slot, target_slot, z, target):
        return pltpu.make_async_remote_copy(
            src_ref=held.at[kind, source_slot, z],
            dst_ref=held.at[kind, target_slot, z],
            send_sem=send_sem.at[kind, path, z],
            recv_sem=recv_sem.at[kind, target_slot, z],
            device_id=target,
            device_id_type=MESH,
        )

    def own_sends(kind, z2):
        c, k, z = view(kind)
        sends = [
            ((z2 <= z) & (z + 1 < depth), 0, k, k, (c, k, z + 1)),
            ((z2 >= z) & (z >= 1), 1, k, k, (c, k, z - 1)),
        ]
        for d in range(1, reach + 1):
            wanted = chip_need(z, d, k, z2)
            if relayed and d == 1:
                inside = (z2 > 0) & (z2 < depth - 1)
                wanted = (c % 2 == 0) & (inside | (z2 == z))
            if relayed and d == 2:
                wanted = wanted | (c % 2 == 1)
            sends.append((wanted, 1 + d, k, 2 * d + k, (c + d, k, z)))
        sends.append((need(1 - k, z, 0, k, z2), 2 + reach, k, k, (c, 1 - k, z)))
        return sends

    def arrival_sends(kind, d, z2):
        c, k, z = view(kind)
        sends = []
        slot = 2 * d + k
        if relayed:
            sends.append(((c % 2 == 1) & (d == 2), 3 + reach, slot, 2 + k, (c - 1, k, z)))
            outer = (c % 2 == 1) & (d == 1) & ((z2 == 0) | (z2 == depth - 1))
            sends.append((outer & (z2 <= z) & (z + 1 < depth),
                          4 + 2 * reach, slot, slot, (c, k, z + 1)))
            sends.append((outer & (z2 >= z) & (z >= 1),
                          5 + 2 * reach, slot, slot, (c, k, z - 1)))
        sends.append((need(1 - k, z, d, k, z2), 3 + reach + d, slot, slot, (c, 1 - k, z)))
        return sends

    def each(kind, sends, z2, finish=False):
        for wanted, path, source_slot, target_slot, target in sends:
            @pl.when(wanted)
            def _():
                moved = copy(kind, path, source_slot, target_slot, z2, device(kind, *target))
                if finish:
                    moved.wait_send()
                else:
                    moved.start()

    def await_block(kind, slot, z2):
        c, k, z = view(kind)
        copy(kind, 0, slot, slot, z2, device(kind, c, 1 - k, z)).wait_recv()

    own = []
    for kind, ref in ((0, text_ref), (1, image_ref)):
        _, k, z = view(kind)
        loaded = pltpu.make_async_copy(ref, held.at[kind, k, z], local_sem.at[kind])
        loaded.start()
        own.append(loaded)

    barrier = pltpu.get_barrier_semaphore()

    def greet(target):
        pl.semaphore_signal(barrier, inc=1, device_id=target, device_id_type=MESH)

    greet((2 * chip + 1 - core, grp))
    if relayed:
        partners = [chip + 1 - 2 * (chip % 2), (chip + 2) % 4]
    else:
        partners = [(chip + d + chips) % chips for d in range(-reach, reach + 1) if d]
    for partner in partners:
        greet((2 * partner + core, grp))

    @pl.when(grp > 0)
    def _():
        greet((blk, grp - 1))

    @pl.when(grp < depth - 1)
    def _():
        greet((blk, grp + 1))

    for loaded in own:
        loaded.wait()
    pl.semaphore_wait(
        barrier,
        1 + len(partners) + (grp > 0).astype(jnp.int32) + (grp < depth - 1).astype(jnp.int32),
    )

    def own_block(kind):
        _, k, z = view(kind)
        return held[kind, k, z]

    def inverse_length(block):
        wide = block.astype(jnp.float32)
        return lax.rsqrt(jnp.sum(wide * wide, axis=-1, keepdims=True) + EPSILON)

    rows = held.shape[3]

    def tile(kind, slot, z2):
        _, k, z = view(kind)
        other = held[kind, slot, z2]
        mine = own_block(1 - kind)
        columns = jnp.broadcast_to(inverse_length(other), (rows, rows)).T
        product = lax.dot_general(
            mine, other, (((1,), (1,)), ((), ())), preferred_element_type=jnp.float32
        )
        logits = LOGIT_SCALE * product * own_scale[kind] * columns + BIAS_LOGIT
        inverse = jnp.exp(-logits)
        weights = 1.0 / (1.0 + inverse)
        diagonal = lax.broadcasted_iota(jnp.int32, (rows, rows), 0) == lax.broadcasted_iota(
            jnp.int32, (rows, rows), 1
        )
        first = ((slot == k) & (z2 == z)).astype(jnp.float32)
        positive = jnp.where(diagonal, first, 0.0)
        weights = jnp.where(positive > 0.5, -inverse * weights, weights)
        scaled = (weights * columns).astype(jnp.bfloat16)
        total[kind] += jnp.dot(scaled, other, preferred_element_type=jnp.float32)

    def position(kind, sign, distance):
        _, _, z = view(kind)
        z2 = z + sign * distance
        valid = (z2 >= 0) & (z2 < depth) & (distance >= 0)
        return z2, valid & ((sign > 0) | (distance > 0))

    def prepare(kind, carry):
        total[kind] = jnp.zeros(total.shape[1:], jnp.float32)
        own_scale[kind] = jnp.broadcast_to(inverse_length(own_block(1 - kind)), (rows, rows))
        return carry

    def start_own(kind):
        _, _, z = view(kind)
        each(kind, own_sends(kind, z), z)

    for kind in kinds:
        start_own(kind)
    lax.fori_loop(0, 2, prepare, 0)

    def half_turn(index, carry):
        turn = index // 2
        kind = first_kind + (index % 2) * (1 - 2 * first_kind)
        _, k, z = view(kind)

        for sign in (1, -1):
            z2, valid = position(kind, sign, turn)

            @pl.when(valid & (turn > 0))
            def _():
                await_block(kind, k, z2)
                each(kind, own_sends(kind, z2), z2)

        def stage(step, carry):
            d = jnp.where(step == 0, reach, jnp.where(step == 1, 0, reach - step + 1))
            distance = turn - (d > 0).astype(jnp.int32)
            for sign in (1, -1):
                z2, valid = position(kind, sign, distance)

                @pl.when((d > 0) & valid & arrives(kind, d, z2))
                def _():
                    await_block(kind, 2 * d + k, z2)
                    each(kind, arrival_sends(kind, d, z2), z2)

            def work(item, carry):
                source_k = (k + item // 2) % 2
                z2, valid = position(kind, 1 - 2 * (item % 2), distance)
                slot = 2 * d + source_k

                @pl.when(valid & need(k, z, d, source_k, z2))
                def _():
                    @pl.when(source_k != k)
                    def _():
                        await_block(kind, slot, z2)

                    tile(kind, slot, z2)

                return carry

            return lax.fori_loop(0, 4, work, carry)

        return lax.fori_loop(0, reach + 1, stage, carry)

    lax.fori_loop(0, 2 * (depth + 1), half_turn, 0)

    for kind, out in ((0, image_out), (1, text_out)):
        scale = own_scale[kind][:, :1]
        unit = own_block(1 - kind).astype(jnp.float32) * scale
        grad = LOGIT_SCALE * total[kind]
        inner = jnp.sum(unit * grad, axis=-1, keepdims=True)
        out[...] = ((grad - unit * inner) * scale).astype(out.dtype)

    def settle(z2, carry):
        for kind in (0, 1):
            each(kind, own_sends(kind, z2), z2, finish=True)
            for d in range(1, reach + 1):
                @pl.when(arrives(kind, d, z2))
                def _():
                    each(kind, arrival_sends(kind, d, z2), z2, finish=True)
        return carry

    lax.fori_loop(0, depth, settle, 0)


def solution(mesh):
    cycle, depth = mesh.shape["blk"], mesh.shape["grp"]
    window = min(20, cycle * depth // 2)
    chips = cycle // 2
    reach = 1
    while (2 * reach + 1) * depth - (depth - 1) < window:
        reach += 1
    slots = 2 * (reach + 1)

    def per_device(image_embeds, text_embeds):
        rows, width = image_embeds.shape
        shape = jax.ShapeDtypeStruct((rows, width), jnp.bfloat16)
        return pl.pallas_call(
            functools.partial(kernel, chips, depth, reach, window),
            out_shape=(shape, shape),
            in_specs=[pl.BlockSpec(memory_space=pl.ANY)] * 2,
            out_specs=(pl.BlockSpec(memory_space=pltpu.VMEM),) * 2,
            scratch_shapes=[
                pltpu.VMEM((2, slots, depth, rows, width), jnp.bfloat16),
                pltpu.VMEM((2, rows, width), jnp.float32),
                pltpu.VMEM((2, rows, rows), jnp.float32),
                pltpu.SemaphoreType.DMA((2,)),
                pltpu.SemaphoreType.DMA((2, 6 + 2 * reach, depth)),
                pltpu.SemaphoreType.DMA((2, slots, depth)),
            ],
            compiler_params=pltpu.CompilerParams(collective_id=0, has_side_effects=True),
        )(image_embeds, text_embeds)

    placed = P(("blk", "grp"), None)
    return jax.shard_map(
        per_device, mesh=mesh, in_specs=(placed, placed), out_specs=(placed, placed), check_vma=False
    )
```

profile of v0, /device:TPU:0, one launch (start us, length us, event | category | flops | bytes accessed | tf_op | source)
XLA Modules:
  0.0 64.6 jit_solution(9079607048903881504)
XLA Ops:
  0.6 61.5 %shard_map.41 = (bf16[128,1152]{1,0:T(8,128)(2,1)}, bf16[128,1152]{1,0:T(8,128)(2,1)}) custom-call(bf16[128,1152]{1,0:T(8,128)(2,1)} %image_ref.1, bf16[128,1152]{1,0:T(8,128)(2,1)} %text_ref.1), custom_call_target="tpu_custom_call" | custom-call | tf_op jit(solution)/shard_map/pallas_call | solution.py:270
  62.1 0.0 copy-start
  62.1 1.7 %copy.6 = bf16[128,1152]{1,0:T(8,128)(2,1)} copy(bf16[128,1152]{1,0:T(8,128)(2,1)} %get-tuple-element.4) | data formatting | bytes 589824
  63.9 0.0 copy-done
  63.9 0.7 %copy.7 = bf16[128,1152]{1,0:T(8,128)(2,1)} copy(bf16[128,1152]{1,0:T(8,128)(2,1)S(1)} %copy-done) | data formatting | bytes 589824
Async XLA Ops:
  62.1 1.8 %copy-start = (bf16[128,1152]{1,0:T(8,128)(2,1)S(1)}, bf16[128,1152]{1,0:T(8,128)(2,1)}, u32[]{:S(2)}) copy-start(bf16[128,1152]{1,0:T(8,128)(2,1)} %get-tuple-element.5) | copy-start | bytes 884740
where the time goes:
time: 65.2 us; the launch traced here: 64.6 us
  Pallas kernels  61.5 us (94%)
  local copies, waits for them, and re-layouts  2.46 us (4%)
    pallas_call x1, Pallas kernels, per_device(): pl.pallas_call(functools.partial(kernel, chips, depth, reach, window), ou...  61.5 us
    unnamed x4, local copies, waits for them, and re-layouts  2.46 us

commit v1 on v0

--- a/solution.py
+++ b/solution.py
@@ -10,6 +10,7 @@
 LOGIT_SCALE = 10.0
 BIAS_LOGIT = -2.0
 EPSILON = 1e-06
+PIECE_ROWS = 16
 MESH = pl.DeviceIdType.MESH
 
 
@@ -255,6 +256,438 @@
     lax.fori_loop(0, depth, settle, 0)
 
 
+def ring_kernel(depth, window, pieces, early, image_ref, text_ref, image_out, text_out,
+                raw, img, txt, own_sum, text_sum, sum_out, sum_in, part_out, part_core, part_x, part_y,
+                load_sem, img_send, img_recv, txt_send, txt_recv, sum_send, sum_recv,
+                part_send, part_recv):
+    blk = lax.axis_index("blk")
+    z = lax.axis_index("grp")
+    chip, core = blk // 2, blk % 2
+    odd = chip % 2
+    rows = raw.shape[1]
+    span = rows // pieces
+    tiles = window // depth
+    is_end = (z == 0) | (z == depth - 1)
+    is_mid = (z > 0) & (z < depth - 1)
+    inner = 1 - 2 * (z // 2)
+    partner = (2 * chip + 1 - core, z)
+    across = (2 * (chip + 1 - 2 * odd) + core, z)
+    over = (2 * ((chip + 2) % 4) + core, z)
+
+    def piece(j):
+        return pl.ds(pl.multiple_of(j * span, span), span)
+
+    def text_rows(slot, j):
+        return pl.ds(pl.multiple_of(slot * rows + j * span, span), span)
+
+    def remote(source, target, send, recv, device):
+        return pltpu.make_async_remote_copy(
+            src_ref=source, dst_ref=target, send_sem=send, recv_sem=recv,
+            device_id=device, device_id_type=MESH,
+        )
+
+    def along(sign):
+        return blk, jnp.minimum(jnp.maximum(z + sign, 0), depth - 1)
+
+    def image_copy(source_z, sign, j):
+        return remote(
+            img.at[source_z, piece(j)], img.at[source_z, piece(j)],
+            img_send.at[(sign + 1) // 2, source_z, j], img_recv.at[source_z, j],
+            along(sign),
+        )
+
+    def sum_copy(target_z, sign, j):
+        return remote(
+            sum_out.at[target_z, piece(j)], sum_in.at[(1 - sign) // 2, target_z, piece(j)],
+            sum_send.at[target_z, j], sum_recv.at[(1 - sign) // 2, target_z, j],
+            along(sign),
+        )
+
+    def text_copy(path, source_slot, target_slot, j, device):
+        return remote(
+            txt.at[text_rows(source_slot, j)], txt.at[text_rows(target_slot, j)],
+            txt_send.at[path, j], txt_recv.at[target_slot, j], device,
+        )
+
+    def text_over(j):
+        return text_copy(0, 0, 4, j, over)
+
+    def text_across(j):
+        return text_copy(1, 4 * odd, 2, j, across)
+
+    def text_core(slot, j):
+        return text_copy(2 + slot // 2, slot, slot + 1 - 2 * core, j, partner)
+
+    def part_copy(path, source_slot, target, j, device):
+        return remote(
+            part_out.at[source_slot, piece(j)], target.at[piece(j)],
+            part_send.at[path, j], part_recv.at[path, j], device,
+        )
+
+    def part_to_core(index, j):
+        return part_copy(index, 2 * index + 1, part_core.at[index], j, partner)
+
+    def part_across(j):
+        return part_copy(2, 2, part_x, j, across)
+
+    def part_over(j):
+        return part_copy(3, 4, part_y, j, over)
+
+    def loop(count, body):
+        def step(j, carry):
+            body(j)
+            return carry
+
+        lax.fori_loop(0, count, step, 0)
+
+    loads = []
+    for kind, ref in ((0, image_ref), (1, text_ref)):
+        load = pltpu.make_async_copy(ref, raw.at[kind], load_sem.at[kind])
+        load.start()
+        loads.append(load)
+
+    barrier = pltpu.get_barrier_semaphore()
+
+    def greet(target):
+        pl.semaphore_signal(barrier, inc=1, device_id=target, device_id_type=MESH)
+
+    for target in (partner, across, over):
+        greet(target)
+
+    @pl.when(z > 0)
+    def _():
+        greet((blk, z - 1))
+
+    @pl.when(z < depth - 1)
+    def _():
+        greet((blk, z + 1))
+
+    def inverse_length(wide):
+        return lax.rsqrt(jnp.sum(wide * wide, axis=-1, keepdims=True) + EPSILON)
+
+    def unit_low(kind):
+        wide = raw[kind].astype(jnp.float32)
+        return (wide * inverse_length(wide)).astype(jnp.bfloat16)
+
+    loads[0].wait()
+    img[z] = unit_low(0)
+    loads[1].wait()
+    txt[pl.ds(0, rows)] = unit_low(1)
+    pl.semaphore_wait(
+        barrier, 3 + (z > 0).astype(jnp.int32) + (z < depth - 1).astype(jnp.int32)
+    )
+
+    @pl.when(is_end)
+    def _():
+        loop(pieces, lambda j: image_copy(z, inner, j).start())
+
+    @pl.when(is_mid)
+    def _():
+        def body(j):
+            image_copy(z, inner, j).start()
+
+            @pl.when(j < early)
+            def _():
+                image_copy(z, -inner, j).start()
+
+        loop(pieces, body)
+
+    def text_start(j):
+        text_over(j).start()
+
+        @pl.when(odd == 0)
+        def _():
+            text_across(j).start()
+
+        @pl.when(core == 0)
+        def _():
+            text_core(0, j).start()
+
+    loop(pieces, text_start)
+    text_sum[...] = jnp.zeros(text_sum.shape, jnp.float32)
+
+    lag = 4 if pieces > 4 else pieces
+
+    def first(j):
+        @pl.when(is_mid & (j < pieces))
+        def _():
+            image_copy(z + inner, -inner, j).wait_recv()
+            image_copy(z + inner, -inner, j).start()
+            image_copy(z - inner, inner, j).wait_recv()
+            image_copy(z - inner, inner, j).start()
+
+        @pl.when(j < pieces)
+        def _():
+            text_copy(0, 0, 4, j, over).wait_recv()
+
+            @pl.when(odd == 1)
+            def _():
+                text_across(j).start()
+
+            @pl.when(core == 1)
+            def _():
+                text_core(4, j).start()
+
+        def second(i):
+            text_copy(1, 0, 2, i, across).wait_recv()
+            text_core(2, i).start()
+
+        @pl.when((odd == 1) & (j < pieces))
+        def _():
+            second(j)
+
+        @pl.when((odd == 0) & (j >= lag))
+        def _():
+            second(j - lag)
+
+    loop(pieces + lag, first)
+
+    def text_ready(j):
+        text_copy(2, 0, 1, j, partner).wait_recv()
+        text_copy(3, 0, 3, j, partner).wait_recv()
+
+    loop(pieces, text_ready)
+
+    def pass_far(low, high):
+        far = z + 2 * inner
+
+        def body(j):
+            image_copy(far, -inner, low + j).wait_recv()
+            image_copy(far, -inner, low + j).start()
+
+        loop(high - low, body)
+
+    def await_image(source_z, low, high):
+        loop(high - low, lambda j: image_copy(source_z, -inner, low + j).wait_recv())
+
+    def weigh(index, carry):
+        @pl.when(is_mid & (index > 0))
+        def _():
+            low = (index - 1) * pieces // 4
+            high = jnp.where(index == 3, pieces, index * pieces // 4)
+            pass_far(low, high)
+
+            @pl.when(index == 3)
+            def _():
+                loop(pieces - early, lambda j: image_copy(z, -inner, early + j).start())
+
+        @pl.when(is_end & (index == 1))
+        def _():
+            await_image(z + 2 * inner, 0, pieces)
+
+        @pl.when(is_end & (index == 2))
+        def _():
+            await_image(z + 3 * inner, 0, pieces)
+
+        @pl.when(is_end & (index == 3))
+        def _():
+            await_image(z + inner, 0, pieces)
+
+        end_step = (index == 1) * 2 + (index == 2) * 3 + (index == 3) * 1
+        mid_step = (index == 1) * 1 - (index == 2) * 1 + (index == 3) * 2
+        source = z + inner * jnp.where(is_end, end_step, mid_step)
+        start = pl.multiple_of(jnp.where(source < z, rows, 0), rows)
+        window_rows = pl.ds(start, tiles * rows)
+        texts = txt[window_rows]
+        image = img[source]
+        product = lax.dot_general(
+            image, texts, (((1,), (1,)), ((), ())), preferred_element_type=jnp.float32
+        )
+        inverse = jnp.exp(-BIAS_LOGIT - LOGIT_SCALE * product)
+        weights = 1.0 / (1.0 + inverse)
+        shape = (rows, tiles * rows)
+        diagonal = lax.broadcasted_iota(jnp.int32, shape, 0) == lax.broadcasted_iota(
+            jnp.int32, shape, 1
+        )
+        positive = jnp.where(diagonal, (index == 0).astype(jnp.float32), 0.0)
+        weights = jnp.where(positive > 0.5, -inverse * weights, weights).astype(jnp.bfloat16)
+        summed = jnp.dot(weights, texts, preferred_element_type=jnp.float32)
+        own_sum[source] = summed
+
+        @pl.when(is_end & (index > 0))
+        def _():
+            sum_out[source] = own_sum[source].astype(jnp.bfloat16)
+            loop(pieces, lambda j: sum_copy(source, inner, j).start())
+
+        text_sum[window_rows] += lax.dot_general(
+            weights, image, (((0,), (0,)), ((), ())), preferred_element_type=jnp.float32
+        )
+        return carry
+
+    lax.fori_loop(0, 4, weigh, 0)
+
+    def relay(target_z, sign, j):
+        arrived = sum_in[(1 - sign) // 2, target_z, piece(j)].astype(jnp.float32)
+        sum_out[target_z, piece(j)] = (own_sum[target_z, piece(j)] + arrived).astype(jnp.bfloat16)
+        sum_copy(target_z, sign, j).start()
+
+    def await_sum(target_z, sign, j):
+        sum_copy(target_z, sign, j).wait_recv()
+
+    def part_rows(slot, j):
+        return text_sum[text_rows(slot, j)]
+
+    def part_first(j):
+        for index in (0, 1):
+            part_out[2 * index + 1, piece(j)] = part_rows(2 * index + 1, j).astype(jnp.bfloat16)
+            part_to_core(index, j).start()
+
+    def part_second(j):
+        for index in (0, 1):
+            part_to_core(index, j).wait_recv()
+        near = part_core[1 - core, piece(j)].astype(jnp.float32)
+        part_out[2, piece(j)] = (part_rows(2, j) + near).astype(jnp.bfloat16)
+        part_across(j).start()
+
+        @pl.when(odd == 0)
+        def _():
+            part_third(j, 0.0)
+
+    def part_third(j, relayed):
+        far = part_core[1, piece(j)].astype(jnp.float32)
+        far = jnp.where(core == 1, far, 0.0) + relayed
+        part_out[4, piece(j)] = (part_rows(4, j) + far).astype(jnp.bfloat16)
+        part_over(j).start()
+
+    def part_fourth(j):
+        part_across(j).wait_recv()
+
+        @pl.when(odd == 1)
+        def _():
+            part_third(j, part_x[piece(j)].astype(jnp.float32))
+
+    loop(pieces, part_first)
+
+    @pl.when(is_mid)
+    def _():
+        def near(j):
+            await_sum(z + inner, inner, j)
+            relay(z + inner, inner, j)
+
+        loop(pieces, near)
+
+    loop(pieces, part_second)
+
+    def middle(j):
+        part_fourth(j)
+
+        @pl.when(is_mid)
+        def _():
+            await_sum(z + 2 * inner, inner, j)
+            relay(z + 2 * inner, inner, j)
+
+    loop(pieces, middle)
+
+    @pl.when(is_mid)
+    def _():
+        def outer(j):
+            await_sum(z - inner, -inner, j)
+            relay(z - inner, -inner, j)
+
+        loop(pieces, outer)
+
+    def finish(kind, out, total, j):
+        wide = raw[kind, piece(j)].astype(jnp.float32)
+        scale = inverse_length(wide)
+        unit = wide * scale
+        grad = LOGIT_SCALE * total
+        radial = jnp.sum(unit * grad, axis=-1, keepdims=True)
+        out[piece(j)] = ((grad - unit * radial) * scale).astype(out.dtype)
+
+    def finish_image(j):
+        await_sum(z, -inner, j)
+        total = own_sum[z, piece(j)] + sum_in[(1 + inner) // 2, z, piece(j)].astype(jnp.float32)
+
+        @pl.when(is_mid)
+        def _():
+            await_sum(z, inner, j)
+
+        other = sum_in[(1 - inner) // 2, z, piece(j)].astype(jnp.float32)
+        finish(0, image_out, total + jnp.where(is_mid, other, 0.0), j)
+
+    def finish_text(j):
+        part_over(j).wait_recv()
+        total = part_rows(0, j) + part_y[piece(j)].astype(jnp.float32)
+        total += jnp.where(core == 0, part_core[0, piece(j)].astype(jnp.float32), 0.0)
+        total += jnp.where(odd == 0, part_x[piece(j)].astype(jnp.float32), 0.0)
+        finish(1, text_out, total, j)
+
+    loop(pieces, finish_text)
+    loop(pieces, finish_image)
+
+    def settle(j):
+        text_over(j).wait_send()
+        text_across(j).wait_send()
+        text_core(2, j).wait_send()
+        part_across(j).wait_send()
+        part_over(j).wait_send()
+        for index in (0, 1):
+            part_to_core(index, j).wait_send()
+
+        @pl.when(core == 0)
+        def _():
+            text_core(0, j).wait_send()
+
+        @pl.when(core == 1)
+        def _():
+            text_core(4, j).wait_send()
+
+        image_copy(z, inner, j).wait_send()
+
+        @pl.when(is_mid)
+        def _():
+            image_copy(z, -inner, j).wait_send()
+            image_copy(z + inner, -inner, j).wait_send()
+            image_copy(z - inner, inner, j).wait_send()
+            image_copy(z + 2 * inner, -inner, j).wait_send()
+            for step, sign in ((1, 1), (2, 1), (-1, -1)):
+                sum_copy(z + step * inner, sign * inner, j).wait_send()
+
+        @pl.when(is_end)
+        def _():
+            for step in (1, 2, 3):
+                sum_copy(z + step * inner, inner, j).wait_send()
+
+    loop(pieces, settle)
+
+
+def square_call(depth, window, image_embeds, text_embeds, shape):
+    rows, width = image_embeds.shape
+    slots = window // depth + 1
+    pieces = rows // PIECE_ROWS
+    early = pieces // 2
+    low, wide = jnp.bfloat16, jnp.float32
+    return pl.pallas_call(
+        functools.partial(ring_kernel, depth, window, pieces, early),
+        out_shape=(shape, shape),
+        in_specs=[pl.BlockSpec(memory_space=pl.ANY)] * 2,
+        out_specs=(pl.BlockSpec(memory_space=pltpu.VMEM),) * 2,
+        scratch_shapes=[
+            pltpu.VMEM((2, rows, width), low),
+            pltpu.VMEM((depth, rows, width), low),
+            pltpu.VMEM((slots * rows, width), low),
+            pltpu.VMEM((depth, rows, width), wide),
+            pltpu.VMEM((slots * rows, width), wide),
+            pltpu.VMEM((depth, rows, width), low),
+            pltpu.VMEM((2, depth, rows, width), low),
+            pltpu.VMEM((slots, rows, width), low),
+            pltpu.VMEM((2, rows, width), low),
+            pltpu.VMEM((rows, width), low),
+            pltpu.VMEM((rows, width), low),
+            pltpu.SemaphoreType.DMA((2,)),
+            pltpu.SemaphoreType.DMA((2, depth, pieces)),
+            pltpu.SemaphoreType.DMA((depth, pieces)),
+            pltpu.SemaphoreType.DMA((5, pieces)),
+            pltpu.SemaphoreType.DMA((slots, pieces)),
+            pltpu.SemaphoreType.DMA((depth, pieces)),
+            pltpu.SemaphoreType.DMA((2, depth, pieces)),
+            pltpu.SemaphoreType.DMA((4, pieces)),
+            pltpu.SemaphoreType.DMA((4, pieces)),
+        ],
+        compiler_params=pltpu.CompilerParams(collective_id=0, has_side_effects=True),
+    )(image_embeds, text_embeds)
+
+
 def solution(mesh):
     cycle, depth = mesh.shape["blk"], mesh.shape["grp"]
     window = min(20, cycle * depth // 2)
@@ -267,6 +700,8 @@
     def per_device(image_embeds, text_embeds):
         rows, width = image_embeds.shape
         shape = jax.ShapeDtypeStruct((rows, width), jnp.bfloat16)
+        if chips == 4 and depth == 4 and window == 4 * depth:
+            return square_call(depth, window, image_embeds, text_embeds, shape)
         return pl.pallas_call(
             functools.partial(kernel, chips, depth, reach, window),
             out_shape=(shape, shape),

time: 65.2 us -> 52 us (0.80)
  Pallas kernels: 61.5 us -> 48.8 us
    pallas_call x1, Pallas kernels: 61.5 us -> 48.8 us  [square_call(): pl.pallas_call(functools.partial(ring_kernel, depth, window, pieces, earl...]
where the time goes in v1:
time: 52 us; the launch traced here: 51.9 us
  Pallas kernels  48.8 us (94%)
  local copies, waits for them, and re-layouts  2.46 us (5%)
  between operations  0.65 us (1%)
    pallas_call x1, Pallas kernels, square_call(): pl.pallas_call(functools.partial(ring_kernel, depth, window, pieces, earl...  48.8 us
    unnamed x4, local copies, waits for them, and re-layouts  2.46 us

profile of v1, /device:TPU:0, one launch (start us, length us, event | category | flops | bytes accessed | tf_op | source)
XLA Modules:
  0.0 51.9 jit_solution(5624495997557120023)
XLA Ops:
  0.6 48.8 %shard_map.41 = (bf16[128,1152]{1,0:T(8,128)(2,1)}, bf16[128,1152]{1,0:T(8,128)(2,1)}) custom-call(bf16[128,1152]{1,0:T(8,128)(2,1)} %image_ref.1, bf16[128,1152]{1,0:T(8,128)(2,1)} %text_ref.1), custom_call_target="tpu_custom_call" | custom-call | tf_op jit(solution)/shard_map/pallas_call | solution.py:660
  49.4 0.0 copy-start
  49.4 1.7 %copy.6 = bf16[128,1152]{1,0:T(8,128)(2,1)} copy(bf16[128,1152]{1,0:T(8,128)(2,1)} %get-tuple-element.4) | data formatting | bytes 589824
  51.2 0.0 copy-done
  51.2 0.7 %copy.7 = bf16[128,1152]{1,0:T(8,128)(2,1)} copy(bf16[128,1152]{1,0:T(8,128)(2,1)S(1)} %copy-done) | data formatting | bytes 589824
Async XLA Ops:
  49.4 1.8 %copy-start = (bf16[128,1152]{1,0:T(8,128)(2,1)S(1)}, bf16[128,1152]{1,0:T(8,128)(2,1)}, u32[]{:S(2)}) copy-start(bf16[128,1152]{1,0:T(8,128)(2,1)} %get-tuple-element.5) | copy-start | bytes 884740

commit v2 on v1

--- a/solution.py
+++ b/solution.py
@@ -10,7 +10,7 @@
 LOGIT_SCALE = 10.0
 BIAS_LOGIT = -2.0
 EPSILON = 1e-06
-PIECE_ROWS = 16
+PIECE_ROWS = 32
 MESH = pl.DeviceIdType.MESH
 
 
@@ -406,16 +406,13 @@
     loop(pieces, text_start)
     text_sum[...] = jnp.zeros(text_sum.shape, jnp.float32)
 
-    lag = 4 if pieces > 4 else pieces
+    lag = pieces
+
+    def pass_image(source_z, sign, j):
+        image_copy(source_z, sign, j).wait_recv()
+        image_copy(source_z, sign, j).start()
 
     def first(j):
-        @pl.when(is_mid & (j < pieces))
-        def _():
-            image_copy(z + inner, -inner, j).wait_recv()
-            image_copy(z + inner, -inner, j).start()
-            image_copy(z - inner, inner, j).wait_recv()
-            image_copy(z - inner, inner, j).start()
-
         @pl.when(j < pieces)
         def _():
             text_copy(0, 0, 4, j, over).wait_recv()
@@ -436,9 +433,18 @@
         def _():
             second(j)
 
+        @pl.when(is_mid & (j < pieces))
+        def _():
+            pass_image(z + inner, -inner, j)
+            pass_image(z - inner, inner, j)
+
         @pl.when((odd == 0) & (j >= lag))
         def _():
             second(j - lag)
+
+        @pl.when(is_mid & (j >= pieces))
+        def _():
+            pass_image(z + 2 * inner, -inner, j - pieces)
 
     loop(pieces + lag, first)
 
@@ -448,24 +454,15 @@
 
     loop(pieces, text_ready)
 
-    def pass_far(low, high):
-        far = z + 2 * inner
-
-        def body(j):
-            image_copy(far, -inner, low + j).wait_recv()
-            image_copy(far, -inner, low + j).start()
-
-        loop(high - low, body)
-
     def await_image(source_z, low, high):
         loop(high - low, lambda j: image_copy(source_z, -inner, low + j).wait_recv())
 
     def weigh(index, carry):
-        @pl.when(is_mid & (index > 0))
-        def _():
-            low = (index - 1) * pieces // 4
-            high = jnp.where(index == 3, pieces, index * pieces // 4)
-            pass_far(low, high)
+        @pl.when(is_mid)
+        def _():
+            low = lag + (pieces - lag) * index // 4
+            high = lag + (pieces - lag) * (index + 1) // 4
+            loop(high - low, lambda j: pass_image(z + 2 * inner, -inner, low + j))
 
             @pl.when(index == 3)
             def _():
@@ -655,11 +652,11 @@
     rows, width = image_embeds.shape
     slots = window // depth + 1
     pieces = rows // PIECE_ROWS
-    early = pieces // 2
+    early = 3 * pieces // 4
     low, wide = jnp.bfloat16, jnp.float32
     return pl.pallas_call(
         functools.partial(ring_kernel, depth, window, pieces, early),
-        out_shape=(shape, shape),
+        out_shape=(pltpu.VMEM(shape.shape, shape.dtype),) * 2,
         in_specs=[pl.BlockSpec(memory_space=pl.ANY)] * 2,
         out_specs=(pl.BlockSpec(memory_space=pltpu.VMEM),) * 2,
         scratch_shapes=[

time: 52 us -> 46.2 us (0.89)
  Pallas kernels: 48.8 us -> 44 us
  local copies, waits for them, and re-layouts: 2.46 us -> 1.43 us
    pallas_call x1, Pallas kernels: 48.8 us -> 44 us  [square_call(): pl.pallas_call(functools.partial(ring_kernel, depth, window, pieces, earl...]
    unnamed x4 -> x2, local copies, waits for them, and re-layouts: 2.46 us -> 1.43 us
where the time goes in v2:
time: 46.2 us; the launch traced here: 46 us
  Pallas kernels  44 us (95%)
  local copies, waits for them, and re-layouts  1.43 us (3%)
  between operations  0.64 us (1%)
    pallas_call x1, Pallas kernels, square_call(): pl.pallas_call(functools.partial(ring_kernel, depth, window, pieces, earl...  44 us
    unnamed x2, local copies, waits for them, and re-layouts  1.43 us

profile of v2, /device:TPU:0, one launch (start us, length us, event | category | flops | bytes accessed | tf_op | source)
XLA Modules:
  0.0 46.0 jit_solution(12839704083046097148)
XLA Ops:
  0.6 44.0 %shard_map.41 = (bf16[128,1152]{1,0:T(8,128)(2,1)S(1)}, bf16[128,1152]{1,0:T(8,128)(2,1)S(1)}) custom-call(bf16[128,1152]{1,0:T(8,128)(2,1)} %image_ref.1, bf16[128,1152]{1,0:T(8,128)(2,1)} %text_ref.1), custom_call_target="tpu_custom_call" | custom-call | tf_op jit(solution)/shard_map/pallas_call | solution.py:657
  44.6 0.7 %copy.6 = bf16[128,1152]{1,0:T(8,128)(2,1)} copy(bf16[128,1152]{1,0:T(8,128)(2,1)S(1)} %get-tuple-element.2) | data formatting | bytes 589824
  45.3 0.7 %copy.7 = bf16[128,1152]{1,0:T(8,128)(2,1)} copy(bf16[128,1152]{1,0:T(8,128)(2,1)S(1)} %get-tuple-element.3) | data formatting | bytes 589824

commit v3 on v0

--- a/solution.py
+++ b/solution.py
@@ -10,6 +10,7 @@
 LOGIT_SCALE = 10.0
 BIAS_LOGIT = -2.0
 EPSILON = 1e-06
+PIECE_ROWS = 32
 MESH = pl.DeviceIdType.MESH
 
 
@@ -255,6 +256,459 @@
     lax.fori_loop(0, depth, settle, 0)
 
 
+def ring_kernel(depth, window, pieces, early, relayed, ahead, image_ref, text_ref, image_out, text_out,
+                raw, img, txt, own_sum, text_sum, weights, sum_out, sum_in, part_out, part_core,
+                part_x, part_y, load_sem, send, image_recv, text_recv, text_core_recv, sum_recv,
+                part_recv, part_core_recv):
+    blk = lax.axis_index("blk")
+    z = lax.axis_index("grp")
+    chip, core = blk // 2, blk % 2
+    odd = chip % 2
+    rows = raw.shape[1]
+    span = rows // pieces
+    columns = window // depth * rows
+    is_end = (z == 0) | (z == depth - 1)
+    is_mid = (z > 0) & (z < depth - 1)
+    inner = 1 - 2 * (z // 2)
+    partner = (2 * chip + 1 - core, z)
+    across = (2 * (chip + 1 - 2 * odd) + core, z)
+    over = (2 * ((chip + 2) % 4) + core, z)
+    corner = (2 * ((chip + 3 - 2 * odd) % 4) + core, z)
+
+    def piece(j):
+        return pl.ds(pl.multiple_of(j * span, span), span)
+
+    def slot_rows(slot, j):
+        return pl.ds(pl.multiple_of(slot * rows + j * span, span), span)
+
+    def remote(source, target, group, recv, device):
+        return pltpu.make_async_remote_copy(
+            src_ref=source, dst_ref=target, send_sem=send.at[group], recv_sem=recv,
+            device_id=device, device_id_type=MESH,
+        )
+
+    def along(sign):
+        return blk, jnp.minimum(jnp.maximum(z + sign, 0), depth - 1)
+
+    def image_copy(source_z, sign, j, group=3):
+        slot = (source_z - z - sign + 2 * depth - 1) % depth
+        return remote(
+            img.at[source_z, piece(j)], img.at[source_z, piece(j)], group,
+            image_recv.at[slot, j], along(sign),
+        )
+
+    def await_image(source_z, j):
+        slot = (source_z - z + 2 * depth - 1) % depth
+        remote(
+            img.at[source_z, piece(j)], img.at[source_z, piece(j)], 3,
+            image_recv.at[slot, j], along(inner),
+        ).wait_recv()
+
+    def pass_image(source_z, sign, j):
+        await_image(source_z, j)
+        image_copy(source_z, sign, j).start()
+
+    def sum_slot(target_z, there, sign):
+        distance = target_z - there
+        distance = jnp.maximum(distance, -distance)
+        return jnp.where(sign == 1 - 2 * (there // 2), distance, depth - 1 + distance)
+
+    def sum_copy(target_z, sign, j):
+        there = along(sign)
+        return remote(
+            sum_out.at[target_z, piece(j)], sum_in.at[(1 - sign) // 2, target_z, piece(j)], 2,
+            sum_recv.at[sum_slot(target_z, there[1], sign), j], there,
+        )
+
+    def await_sum(target_z, sign, j):
+        remote(
+            sum_out.at[target_z, piece(j)], sum_in.at[(1 - sign) // 2, target_z, piece(j)], 2,
+            sum_recv.at[sum_slot(target_z, z, sign), j], along(inner),
+        ).wait_recv()
+
+    def text_copy(source_slot, target_slot, recv, j, device):
+        return remote(
+            txt.at[slot_rows(source_slot, j)], txt.at[slot_rows(target_slot, j)], 0, recv, device
+        )
+
+    def text_over(j):
+        return text_copy(0, 4, text_recv.at[1, j], j, over)
+
+    def text_across(j):
+        return text_copy(4 * odd, 2, text_recv.at[0, j], j, across)
+
+    def text_corner(j):
+        return text_copy(0, 2, text_recv.at[0, j], j, corner)
+
+    def text_to_core(slot, j):
+        target = slot + 1 - 2 * core
+        return text_copy(slot, target, text_core_recv.at[target // 2], j, partner)
+
+    def part_to_core(index, j):
+        return remote(
+            part_out.at[2 * index + 1, piece(j)], part_core.at[index, piece(j)], 1,
+            part_core_recv.at[j], partner,
+        )
+
+    def part_across(j):
+        return remote(
+            part_out.at[2, piece(j)], part_x.at[piece(j)], 1, part_recv.at[0, j], across
+        )
+
+    def part_corner(j):
+        return remote(
+            part_out.at[2, piece(j)], part_x.at[piece(j)], 1, part_recv.at[0, j], corner
+        )
+
+    def part_over(j):
+        return remote(
+            part_out.at[4, piece(j)], part_y.at[piece(j)], 1, part_recv.at[1, j], over
+        )
+
+    def span_loop(low, high, body):
+        def step(j, carry):
+            body(j)
+            return carry
+
+        lax.fori_loop(low, high, step, 0)
+
+    def loop(count, body):
+        span_loop(0, count, body)
+
+    loads = []
+    for kind, ref in ((0, image_ref), (1, text_ref)):
+        load = pltpu.make_async_copy(ref, raw.at[kind], load_sem.at[kind])
+        load.start()
+        loads.append(load)
+
+    barrier = pltpu.get_barrier_semaphore()
+
+    def greet(target):
+        pl.semaphore_signal(barrier, inc=1, device_id=target, device_id_type=MESH)
+
+    for target in (partner, across, over, corner):
+        greet(target)
+
+    @pl.when(z > 0)
+    def _():
+        greet((blk, z - 1))
+
+    @pl.when(z < depth - 1)
+    def _():
+        greet((blk, z + 1))
+
+    def inverse_length(wide):
+        return lax.rsqrt(jnp.sum(wide * wide, axis=-1, keepdims=True) + EPSILON)
+
+    def unit_low(kind):
+        wide = raw[kind].astype(jnp.float32)
+        return (wide * inverse_length(wide)).astype(jnp.bfloat16)
+
+    loads[0].wait()
+    img[z] = unit_low(0)
+    loads[1].wait()
+    txt[pl.ds(0, rows)] = unit_low(1)
+    pl.semaphore_wait(
+        barrier, 4 + (z > 0).astype(jnp.int32) + (z < depth - 1).astype(jnp.int32)
+    )
+
+    def image_start(j):
+        image_copy(z, inner, j, 2).start()
+
+        @pl.when(is_mid & (j < early))
+        def _():
+            image_copy(z, -inner, j).start()
+
+    def text_start(j):
+        text_over(j).start()
+
+        @pl.when(odd == 0)
+        def _():
+            text_across(j).start()
+
+        @pl.when((odd == 1) & (j >= relayed))
+        def _():
+            text_corner(j).start()
+
+        @pl.when(core == 0)
+        def _():
+            text_to_core(0, j).start()
+
+    loop(pieces, image_start)
+    loop(pieces, text_start)
+    text_sum[...] = jnp.zeros(text_sum.shape, jnp.float32)
+
+    def first(j):
+        @pl.when(j < pieces)
+        def _():
+            text_over(j).wait_recv()
+
+            @pl.when((odd == 1) & (j < relayed))
+            def _():
+                text_across(j).start()
+
+            @pl.when(core == 1)
+            def _():
+                text_to_core(4, j).start()
+
+        def second(i):
+            text_across(i).wait_recv()
+            text_to_core(2, i).start()
+
+        @pl.when((odd == 1) & (j < pieces))
+        def _():
+            second(j)
+
+        @pl.when(is_mid & (j < pieces))
+        def _():
+            pass_image(z + inner, -inner, j)
+            pass_image(z - inner, inner, j)
+
+        @pl.when((odd == 0) & (j >= ahead))
+        def _():
+            second(j - ahead)
+
+        @pl.when(is_mid & (j >= pieces))
+        def _():
+            pass_image(z + 2 * inner, -inner, j - pieces)
+
+    loop(pieces + ahead, first)
+    for index in (0, 1):
+        slot = 2 * index + 1
+        block = txt.at[pl.ds(slot * rows, rows)]
+        remote(block, block, 0, text_core_recv.at[index], partner).wait_recv()
+
+    def text_window(source):
+        start = pl.multiple_of(jnp.where(source < z, rows, 0), rows)
+        return pl.ds(start, columns)
+
+    def weigh(source, start, count):
+        some = pl.ds(start, count)
+        texts = txt[text_window(source)]
+        product = lax.dot_general(
+            img[source, some], texts, (((1,), (1,)), ((), ())), preferred_element_type=jnp.float32
+        )
+        inverse = jnp.exp(-BIAS_LOGIT - LOGIT_SCALE * product)
+        slope = 1.0 / (1.0 + inverse)
+        shape = (count, columns)
+        diagonal = lax.broadcasted_iota(jnp.int32, shape, 0) + start == lax.broadcasted_iota(
+            jnp.int32, shape, 1
+        )
+        positive = jnp.where(diagonal, (source == z).astype(jnp.float32), 0.0)
+        slope = jnp.where(positive > 0.5, -inverse * slope, slope).astype(jnp.bfloat16)
+        weights[source, some] = slope
+        own_sum[source, some] = jnp.dot(slope, texts, preferred_element_type=jnp.float32)
+
+    def add_texts(source):
+        text_sum[text_window(source)] += lax.dot_general(
+            weights[source], img[source], (((0,), (0,)), ((), ())),
+            preferred_element_type=jnp.float32,
+        )
+
+    def relay(target_z, sign, j):
+        await_sum(target_z, sign, j)
+        arrived = sum_in[(1 - sign) // 2, target_z, piece(j)].astype(jnp.float32)
+        sum_out[target_z, piece(j)] = (own_sum[target_z, piece(j)] + arrived).astype(jnp.bfloat16)
+        sum_copy(target_z, sign, j).start()
+
+    def near(j):
+        relay(z + inner, inner, j)
+
+    @pl.when(is_end)
+    def _():
+        group = pieces // 2
+
+        def half_step(index):
+            step = (index % 3 == 0) * 2 - (index == 6) + (index == 4) * 3 + (index == 5) * 3
+            step += (index == 7)
+            source = z + step * inner
+            half = (index == 2) + (index % 2) * (index > 2)
+            start = half * group
+
+            @pl.when(step > 0)
+            def _():
+                loop(group, lambda j: await_image(source, start + j))
+
+            weigh(source, pl.multiple_of(start * span, group * span), group * span)
+
+            @pl.when(step > 0)
+            def _():
+                some = pl.ds(pl.multiple_of(start * span, group * span), group * span)
+                sum_out[source, some] = own_sum[source, some].astype(jnp.bfloat16)
+                loop(group, lambda j: sum_copy(source, inner, start + j).start())
+
+            @pl.when(half == 1)
+            def _():
+                add_texts(source)
+
+        loop(8, half_step)
+
+    @pl.when(is_mid)
+    def _():
+        half = (ahead + pieces) // 2
+
+        def image_step(index):
+            def far(j):
+                pass_image(z + 2 * inner, -inner, j)
+
+            @pl.when(index == 1)
+            def _():
+                span_loop(ahead, half, far)
+
+            @pl.when(index == 2)
+            def _():
+                span_loop(half, pieces, far)
+                span_loop(early, pieces, lambda j: image_copy(z, -inner, j).start())
+                span_loop(0, pieces // 4, near)
+
+            @pl.when(index == 3)
+            def _():
+                span_loop(pieces // 4, pieces // 2, near)
+
+            step = (index == 0) * 1 - (index == 1) * 1 + (index == 3) * 2
+            source = z + step * inner
+            weigh(source, 0, rows)
+            add_texts(source)
+
+        loop(4, image_step)
+
+    def part_rows(slot, j):
+        return text_sum[slot_rows(slot, j)]
+
+    def part_first(j):
+        for index in (0, 1):
+            slot = 2 * index + 1
+            part_out[slot, piece(j)] = part_rows(slot, j).astype(jnp.bfloat16)
+            part_to_core(index, j).start()
+
+    def part_second(j):
+        pair = part_core.at[0, pl.ds(0, 2 * span)]
+        remote(pair, pair, 1, part_core_recv.at[j], partner).wait_recv()
+        side = part_core[1 - core, piece(j)].astype(jnp.float32)
+        part_out[2, piece(j)] = (part_rows(2, j) + side).astype(jnp.bfloat16)
+
+        @pl.when((odd == 1) | (j < relayed))
+        def _():
+            part_across(j).start()
+
+        @pl.when((odd == 0) & (j >= relayed))
+        def _():
+            part_corner(j).start()
+
+        @pl.when((odd == 0) | (j >= relayed))
+        def _():
+            part_third(j, 0.0)
+
+    def part_third(j, arrived):
+        side = part_core[1, piece(j)].astype(jnp.float32)
+        side = jnp.where(core == 1, side, 0.0) + arrived
+        part_out[4, piece(j)] = (part_rows(4, j) + side).astype(jnp.bfloat16)
+        part_over(j).start()
+
+    loop(pieces, part_first)
+
+    @pl.when(is_mid)
+    def _():
+        span_loop(pieces // 2, pieces, near)
+
+    loop(pieces, part_second)
+
+    def middle(j):
+        @pl.when(is_mid)
+        def _():
+            relay(z + 2 * inner, inner, j)
+
+        part_across(j).wait_recv()
+
+        @pl.when((odd == 1) & (j < relayed))
+        def _():
+            part_third(j, part_x[piece(j)].astype(jnp.float32))
+
+    loop(pieces, middle)
+
+    @pl.when(is_mid)
+    def _():
+        loop(pieces, lambda j: relay(z - inner, -inner, j))
+
+    def finish(kind, out, total, j):
+        wide = raw[kind, piece(j)].astype(jnp.float32)
+        scale = inverse_length(wide)
+        unit = wide * scale
+        grad = LOGIT_SCALE * total
+        radial = jnp.sum(unit * grad, axis=-1, keepdims=True)
+        out[piece(j)] = ((grad - unit * radial) * scale).astype(out.dtype)
+
+    def finish_text(j):
+        part_over(j).wait_recv()
+        total = part_rows(0, j) + part_y[piece(j)].astype(jnp.float32)
+        total += jnp.where(core == 0, part_core[0, piece(j)].astype(jnp.float32), 0.0)
+        total += jnp.where(
+            (odd == 0) | (j >= relayed), part_x[piece(j)].astype(jnp.float32), 0.0
+        )
+        finish(1, text_out, total, j)
+
+    def finish_image(j):
+        await_sum(z, -inner, j)
+        total = own_sum[z, piece(j)] + sum_in[(1 + inner) // 2, z, piece(j)].astype(jnp.float32)
+
+        @pl.when(is_mid)
+        def _():
+            await_sum(z, inner, j)
+
+        other = sum_in[(1 - inner) // 2, z, piece(j)].astype(jnp.float32)
+        finish(0, image_out, total + jnp.where(is_mid, other, 0.0), j)
+
+    loop(pieces, finish_text)
+    loop(pieces, finish_image)
+
+    def settle(group):
+        remote(img, img, group, image_recv.at[0, 0], partner).wait_send()
+
+    for group in (0, 1, 2):
+        settle(group)
+
+    @pl.when(is_mid)
+    def _():
+        settle(3)
+
+
+def square_call(depth, window, image_embeds, text_embeds):
+    rows, width = image_embeds.shape
+    slots = window // depth + 1
+    pieces = rows // PIECE_ROWS
+    early, relayed, ahead = 3 * pieces // 4, 3 * pieces // 4, pieces // 2
+    low, wide = jnp.bfloat16, jnp.float32
+    return pl.pallas_call(
+        functools.partial(ring_kernel, depth, window, pieces, early, relayed, ahead),
+        out_shape=(pltpu.VMEM((rows, width), low),) * 2,
+        in_specs=[pl.BlockSpec(memory_space=pl.ANY)] * 2,
+        out_specs=(pl.BlockSpec(memory_space=pltpu.VMEM),) * 2,
+        scratch_shapes=[
+            pltpu.VMEM((2, rows, width), low),
+            pltpu.VMEM((depth, rows, width), low),
+            pltpu.VMEM((slots * rows, width), low),
+            pltpu.VMEM((depth, rows, width), wide),
+            pltpu.VMEM((slots * rows, width), wide),
+            pltpu.VMEM((depth, rows, (slots - 1) * rows), low),
+            pltpu.VMEM((depth, rows, width), low),
+            pltpu.VMEM((2, depth, rows, width), low),
+            pltpu.VMEM((slots, rows, width), low),
+            pltpu.VMEM((2, rows, width), low),
+            pltpu.VMEM((rows, width), low),
+            pltpu.VMEM((rows, width), low),
+            pltpu.SemaphoreType.DMA((2,)),
+            pltpu.SemaphoreType.DMA((4,)),
+            pltpu.SemaphoreType.DMA((depth - 1, pieces)),
+            pltpu.SemaphoreType.DMA((2, pieces)),
+            pltpu.SemaphoreType.DMA((2,)),
+            pltpu.SemaphoreType.DMA((depth + 1, pieces)),
+            pltpu.SemaphoreType.DMA((2, pieces)),
+            pltpu.SemaphoreType.DMA((pieces,)),
+        ],
+        compiler_params=pltpu.CompilerParams(collective_id=0, has_side_effects=True),
+    )(image_embeds, text_embeds)
+
+
 def solution(mesh):
     cycle, depth = mesh.shape["blk"], mesh.shape["grp"]
     window = min(20, cycle * depth // 2)
@@ -267,6 +721,8 @@
     def per_device(image_embeds, text_embeds):
         rows, width = image_embeds.shape
         shape = jax.ShapeDtypeStruct((rows, width), jnp.bfloat16)
+        if chips == 4 and depth == 4 and window == 4 * depth:
+            return square_call(depth, window, image_embeds, text_embeds)
         return pl.pallas_call(
             functools.partial(kernel, chips, depth, reach, window),
             out_shape=(shape, shape),

time: 65.2 us -> 42.9 us (0.66)
  Pallas kernels: 61.5 us -> 40.6 us
  local copies, waits for them, and re-layouts: 2.46 us -> 1.43 us
    pallas_call x1, Pallas kernels: 61.5 us -> 40.6 us  [square_call(): pl.pallas_call(functools.partial(ring_kernel, depth, window, pieces, earl...]
    unnamed x4 -> x2, local copies, waits for them, and re-layouts: 2.46 us -> 1.43 us
where the time goes in v3:
time: 42.9 us; the launch traced here: 42.6 us
  Pallas kernels  40.6 us (95%)
  local copies, waits for them, and re-layouts  1.43 us (3%)
  between operations  0.64 us (1%)
    pallas_call x1, Pallas kernels, square_call(): pl.pallas_call(functools.partial(ring_kernel, depth, window, pieces, earl...  40.6 us
    unnamed x2, local copies, waits for them, and re-layouts  1.43 us

profile of v3, /device:TPU:0, one launch (start us, length us, event | category | flops | bytes accessed | tf_op | source)
XLA Modules:
  0.0 42.6 jit_solution(11737248325539952384)
XLA Ops:
  0.6 40.6 %shard_map.41 = (bf16[128,1152]{1,0:T(8,128)(2,1)S(1)}, bf16[128,1152]{1,0:T(8,128)(2,1)S(1)}) custom-call(bf16[128,1152]{1,0:T(8,128)(2,1)} %image_ref.1, bf16[128,1152]{1,0:T(8,128)(2,1)} %text_ref.1), custom_call_target="tpu_custom_call" | custom-call | tf_op jit(solution)/shard_map/pallas_call | solution.py:681
  41.2 0.7 %copy.6 = bf16[128,1152]{1,0:T(8,128)(2,1)} copy(bf16[128,1152]{1,0:T(8,128)(2,1)S(1)} %get-tuple-element.2) | data formatting | bytes 589824
  41.9 0.7 %copy.7 = bf16[128,1152]{1,0:T(8,128)(2,1)} copy(bf16[128,1152]{1,0:T(8,128)(2,1)S(1)} %get-tuple-element.3) | data formatting | bytes 589824

commit v4 on v3

--- a/solution.py
+++ b/solution.py
@@ -266,6 +266,7 @@
     odd = chip % 2
     rows = raw.shape[1]
     span = rows // pieces
+    parts, part_span = 2 * pieces, span // 2
     columns = window // depth * rows
     is_end = (z == 0) | (z == depth - 1)
     is_mid = (z > 0) & (z < depth - 1)
@@ -278,6 +279,9 @@
     def piece(j):
         return pl.ds(pl.multiple_of(j * span, span), span)
 
+    def part(j):
+        return pl.ds(pl.multiple_of(j * part_span, part_span), part_span)
+
     def slot_rows(slot, j):
         return pl.ds(pl.multiple_of(slot * rows + j * span, span), span)
 
@@ -346,23 +350,23 @@
 
     def part_to_core(index, j):
         return remote(
-            part_out.at[2 * index + 1, piece(j)], part_core.at[index, piece(j)], 1,
+            part_out.at[2 * index + 1, part(j)], part_core.at[index, part(j)], 1,
             part_core_recv.at[j], partner,
         )
 
     def part_across(j):
         return remote(
-            part_out.at[2, piece(j)], part_x.at[piece(j)], 1, part_recv.at[0, j], across
+            part_out.at[2, part(j)], part_x.at[part(j)], 1, part_recv.at[0, j], across
         )
 
     def part_corner(j):
         return remote(
-            part_out.at[2, piece(j)], part_x.at[piece(j)], 1, part_recv.at[0, j], corner
+            part_out.at[2, part(j)], part_x.at[part(j)], 1, part_recv.at[0, j], corner
         )
 
     def part_over(j):
         return remote(
-            part_out.at[4, piece(j)], part_y.at[piece(j)], 1, part_recv.at[1, j], over
+            part_out.at[4, part(j)], part_y.at[part(j)], 1, part_recv.at[1, j], over
         )
 
     def span_loop(low, high, body):
@@ -499,10 +503,11 @@
         weights[source, some] = slope
         own_sum[source, some] = jnp.dot(slope, texts, preferred_element_type=jnp.float32)
 
-    def add_texts(source):
-        text_sum[text_window(source)] += lax.dot_general(
-            weights[source], img[source], (((0,), (0,)), ((), ())),
-            preferred_element_type=jnp.float32,
+    def add_texts(*sources):
+        slopes = jnp.concatenate([weights[source] for source in sources])
+        images = jnp.concatenate([img[source] for source in sources])
+        text_sum[text_window(sources[0])] += lax.dot_general(
+            slopes, images, (((0,), (0,)), ((), ())), preferred_element_type=jnp.float32
         )
 
     def relay(target_z, sign, j):
@@ -517,31 +522,34 @@
     @pl.when(is_end)
     def _():
         group = pieces // 2
-
-        def half_step(index):
-            step = (index % 3 == 0) * 2 - (index == 6) + (index == 4) * 3 + (index == 5) * 3
-            step += (index == 7)
-            source = z + step * inner
-            half = (index == 2) + (index % 2) * (index > 2)
-            start = half * group
-
-            @pl.when(step > 0)
-            def _():
-                loop(group, lambda j: await_image(source, start + j))
-
-            weigh(source, pl.multiple_of(start * span, group * span), group * span)
-
-            @pl.when(step > 0)
-            def _():
-                some = pl.ds(pl.multiple_of(start * span, group * span), group * span)
-                sum_out[source, some] = own_sum[source, some].astype(jnp.bfloat16)
-                loop(group, lambda j: sum_copy(source, inner, start + j).start())
-
-            @pl.when(half == 1)
-            def _():
-                add_texts(source)
-
-        loop(8, half_step)
+        near_z, far_z, edge_z = z + 2 * inner, z + 3 * inner, z + inner
+
+        def take(source, low, count):
+            span_loop(low, low + count, lambda j: await_image(source, j))
+            weigh(source, pl.multiple_of(low * span, count * span), count * span)
+            some = pl.ds(pl.multiple_of(low * span, count * span), count * span)
+            sum_out[source, some] = own_sum[source, some].astype(jnp.bfloat16)
+
+        def give(source, low, high):
+            span_loop(low, high, lambda j: sum_copy(source, inner, j).start())
+
+        def far_step(j):
+            take(far_z, j, 1)
+            give(far_z, j, j + 1)
+
+        take(near_z, 0, group)
+        give(near_z, 0, group)
+        weigh(z, 0, rows)
+        add_texts(z)
+        take(near_z, group, group)
+        give(near_z, group, pieces - 1)
+        add_texts(near_z)
+        take(edge_z, 0, group)
+        loop(pieces, far_step)
+        give(near_z, pieces - 1, pieces)
+        take(edge_z, group, group)
+        give(edge_z, 0, pieces)
+        add_texts(far_z, edge_z)
 
     @pl.when(is_mid)
     def _():
@@ -573,62 +581,69 @@
         loop(4, image_step)
 
     def part_rows(slot, j):
-        return text_sum[slot_rows(slot, j)]
+        return text_sum[pl.ds(pl.multiple_of(slot * rows + j * part_span, part_span), part_span)]
 
     def part_first(j):
         for index in (0, 1):
             slot = 2 * index + 1
-            part_out[slot, piece(j)] = part_rows(slot, j).astype(jnp.bfloat16)
+            part_out[slot, part(j)] = part_rows(slot, j).astype(jnp.bfloat16)
             part_to_core(index, j).start()
 
     def part_second(j):
-        pair = part_core.at[0, pl.ds(0, 2 * span)]
+        pair = part_core.at[0, pl.ds(0, 2 * part_span)]
         remote(pair, pair, 1, part_core_recv.at[j], partner).wait_recv()
-        side = part_core[1 - core, piece(j)].astype(jnp.float32)
-        part_out[2, piece(j)] = (part_rows(2, j) + side).astype(jnp.bfloat16)
-
-        @pl.when((odd == 1) | (j < relayed))
+        side = part_core[1 - core, part(j)].astype(jnp.float32)
+        part_out[2, part(j)] = (part_rows(2, j) + side).astype(jnp.bfloat16)
+
+        @pl.when((odd == 1) | (j < 2 * relayed))
         def _():
             part_across(j).start()
 
-        @pl.when((odd == 0) & (j >= relayed))
+        @pl.when((odd == 0) & (j >= 2 * relayed))
         def _():
             part_corner(j).start()
 
-        @pl.when((odd == 0) | (j >= relayed))
+        @pl.when((odd == 0) | (j >= 2 * relayed))
         def _():
             part_third(j, 0.0)
 
     def part_third(j, arrived):
-        side = part_core[1, piece(j)].astype(jnp.float32)
+        side = part_core[1, part(j)].astype(jnp.float32)
         side = jnp.where(core == 1, side, 0.0) + arrived
-        part_out[4, piece(j)] = (part_rows(4, j) + side).astype(jnp.bfloat16)
+        part_out[4, part(j)] = (part_rows(4, j) + side).astype(jnp.bfloat16)
         part_over(j).start()
 
-    loop(pieces, part_first)
+    def part_relay(j):
+        part_across(j).wait_recv()
+        part_third(j, part_x[part(j)].astype(jnp.float32))
+
+    loop(parts, part_first)
 
     @pl.when(is_mid)
     def _():
-        span_loop(pieces // 2, pieces, near)
-
-    loop(pieces, part_second)
-
-    def middle(j):
+        span_loop(pieces // 2, pieces - 1, near)
+
+    loop(parts, part_second)
+
+    @pl.when(is_mid)
+    def _():
+        loop(pieces, lambda j: relay(z + 2 * inner, inner, j))
+
+    def outer(j):
+        @pl.when((odd == 1) & (j < relayed))
+        def _():
+            part_relay(2 * j)
+            part_relay(2 * j + 1)
+
         @pl.when(is_mid)
         def _():
-            relay(z + 2 * inner, inner, j)
-
-        part_across(j).wait_recv()
-
-        @pl.when((odd == 1) & (j < relayed))
-        def _():
-            part_third(j, part_x[piece(j)].astype(jnp.float32))
-
-    loop(pieces, middle)
-
-    @pl.when(is_mid)
-    def _():
-        loop(pieces, lambda j: relay(z - inner, -inner, j))
+            relay(z - inner, -inner, j)
+
+            @pl.when(j == 1)
+            def _():
+                near(pieces - 1)
+
+    loop(pieces, outer)
 
     def finish(kind, out, total, j):
         wide = raw[kind, piece(j)].astype(jnp.float32)
@@ -639,12 +654,17 @@
         out[piece(j)] = ((grad - unit * radial) * scale).astype(out.dtype)
 
     def finish_text(j):
-        part_over(j).wait_recv()
-        total = part_rows(0, j) + part_y[piece(j)].astype(jnp.float32)
+        direct = (odd == 0) | (j >= relayed)
+        for half in (0, 1):
+            part_over(2 * j + half).wait_recv()
+
+            @pl.when(direct)
+            def _():
+                part_across(2 * j + half).wait_recv()
+
+        total = text_sum[slot_rows(0, j)] + part_y[piece(j)].astype(jnp.float32)
         total += jnp.where(core == 0, part_core[0, piece(j)].astype(jnp.float32), 0.0)
-        total += jnp.where(
-            (odd == 0) | (j >= relayed), part_x[piece(j)].astype(jnp.float32), 0.0
-        )
+        total += jnp.where(direct, part_x[piece(j)].astype(jnp.float32), 0.0)
         finish(1, text_out, total, j)
 
     def finish_image(j):
@@ -658,8 +678,11 @@
         other = sum_in[(1 - inner) // 2, z, piece(j)].astype(jnp.float32)
         finish(0, image_out, total + jnp.where(is_mid, other, 0.0), j)
 
-    loop(pieces, finish_text)
-    loop(pieces, finish_image)
+    def finish_both(j):
+        finish_image(j)
+        finish_text(j)
+
+    loop(pieces, finish_both)
 
     def settle(group):
         remote(img, img, group, image_recv.at[0, 0], partner).wait_send()
@@ -702,8 +725,8 @@
             pltpu.SemaphoreType.DMA((2, pieces)),
             pltpu.SemaphoreType.DMA((2,)),
             pltpu.SemaphoreType.DMA((depth + 1, pieces)),
-            pltpu.SemaphoreType.DMA((2, pieces)),
-            pltpu.SemaphoreType.DMA((pieces,)),
+            pltpu.SemaphoreType.DMA((2, 2 * pieces)),
+            pltpu.SemaphoreType.DMA((2 * pieces,)),
         ],
         compiler_params=pltpu.CompilerParams(collective_id=0, has_side_effects=True),
     )(image_embeds, text_embeds)

time: 42.9 us -> 41 us (0.956)
  Pallas kernels: 40.6 us -> 38.8 us
    pallas_call x1, Pallas kernels: 40.6 us -> 38.8 us  [square_call(): pl.pallas_call(functools.partial(ring_kernel, depth, window, pieces, earl...]
where the time goes in v4:
time: 41 us; the launch traced here: 40.9 us
  Pallas kernels  38.8 us (95%)
  local copies, waits for them, and re-layouts  1.43 us (3%)
  between operations  0.64 us (2%)
    pallas_call x1, Pallas kernels, square_call(): pl.pallas_call(functools.partial(ring_kernel, depth, window, pieces, earl...  38.8 us
    unnamed x2, local copies, waits for them, and re-layouts  1.43 us

profile of v4, /device:TPU:0, one launch (start us, length us, event | category | flops | bytes accessed | tf_op | source)
XLA Modules:
  0.0 40.9 jit_solution(15168173756394829283)
XLA Ops:
  0.6 38.8 %shard_map.41 = (bf16[128,1152]{1,0:T(8,128)(2,1)S(1)}, bf16[128,1152]{1,0:T(8,128)(2,1)S(1)}) custom-call(bf16[128,1152]{1,0:T(8,128)(2,1)} %image_ref.1, bf16[128,1152]{1,0:T(8,128)(2,1)} %text_ref.1), custom_call_target="tpu_custom_call" | custom-call | tf_op jit(solution)/shard_map/pallas_call | solution.py:704
  39.4 0.7 %copy.6 = bf16[128,1152]{1,0:T(8,128)(2,1)} copy(bf16[128,1152]{1,0:T(8,128)(2,1)S(1)} %get-tuple-element.2) | data formatting | bytes 589824
  40.2 0.7 %copy.7 = bf16[128,1152]{1,0:T(8,128)(2,1)} copy(bf16[128,1152]{1,0:T(8,128)(2,1)S(1)} %get-tuple-element.3) | data formatting | bytes 589824

commit v5 on v4

--- a/solution.py
+++ b/solution.py
@@ -256,7 +256,7 @@
     lax.fori_loop(0, depth, settle, 0)
 
 
-def ring_kernel(depth, window, pieces, early, relayed, ahead, image_ref, text_ref, image_out, text_out,
+def ring_kernel(depth, window, pieces, early, relayed, passed, ahead, image_ref, text_ref, image_out, text_out,
                 raw, img, txt, own_sum, text_sum, weights, sum_out, sum_in, part_out, part_core,
                 part_x, part_y, load_sem, send, image_recv, text_recv, text_core_recv, sum_recv,
                 part_recv, part_core_recv):
@@ -271,6 +271,8 @@
     is_end = (z == 0) | (z == depth - 1)
     is_mid = (z > 0) & (z < depth - 1)
     inner = 1 - 2 * (z // 2)
+    bare = (z == 0) & (core == 0)
+    passed = jnp.where(bare, 0, passed)
     partner = (2 * chip + 1 - core, z)
     across = (2 * (chip + 1 - 2 * odd) + core, z)
     over = (2 * ((chip + 2) % 4) + core, z)
@@ -320,13 +322,13 @@
     def sum_copy(target_z, sign, j):
         there = along(sign)
         return remote(
-            sum_out.at[target_z, piece(j)], sum_in.at[(1 - sign) // 2, target_z, piece(j)], 2,
+            sum_out.at[target_z, part(j)], sum_in.at[(1 - sign) // 2, target_z, part(j)], 2,
             sum_recv.at[sum_slot(target_z, there[1], sign), j], there,
         )
 
     def await_sum(target_z, sign, j):
         remote(
-            sum_out.at[target_z, piece(j)], sum_in.at[(1 - sign) // 2, target_z, piece(j)], 2,
+            sum_out.at[target_z, part(j)], sum_in.at[(1 - sign) // 2, target_z, part(j)], 2,
             sum_recv.at[sum_slot(target_z, z, sign), j], along(inner),
         ).wait_recv()
 
@@ -417,7 +419,9 @@
     )
 
     def image_start(j):
-        image_copy(z, inner, j, 2).start()
+        @pl.when(is_end | (j < early))
+        def _():
+            image_copy(z, inner, j, 2).start()
 
         @pl.when(is_mid & (j < early))
         def _():
@@ -442,6 +446,12 @@
     loop(pieces, text_start)
     text_sum[...] = jnp.zeros(text_sum.shape, jnp.float32)
 
+    def pass_inner(q):
+        late = q >= early + pieces
+        from_far = (q >= early) & (q < early + pieces)
+        j = q - jnp.where(late, pieces, jnp.where(from_far, early, 0))
+        pass_image(z + inner * (1 + from_far), -inner, j)
+
     def first(j):
         @pl.when(j < pieces)
         def _():
@@ -463,18 +473,21 @@
         def _():
             second(j)
 
-        @pl.when(is_mid & (j < pieces))
-        def _():
-            pass_image(z + inner, -inner, j)
-            pass_image(z - inner, inner, j)
+        @pl.when(is_mid)
+        def _():
+            pass_inner(j)
+
+            @pl.when(j < pieces)
+            def _():
+                pass_image(z - inner, inner, j)
+
+            @pl.when(j == pieces - 1)
+            def _():
+                span_loop(early, pieces, lambda i: image_copy(z, inner, i, 2).start())
 
         @pl.when((odd == 0) & (j >= ahead))
         def _():
             second(j - ahead)
-
-        @pl.when(is_mid & (j >= pieces))
-        def _():
-            pass_image(z + 2 * inner, -inner, j - pieces)
 
     loop(pieces + ahead, first)
     for index in (0, 1):
@@ -486,11 +499,11 @@
         start = pl.multiple_of(jnp.where(source < z, rows, 0), rows)
         return pl.ds(start, columns)
 
-    def weigh(source, start, count):
+    def slopes_of(source, start, count):
         some = pl.ds(start, count)
-        texts = txt[text_window(source)]
         product = lax.dot_general(
-            img[source, some], texts, (((1,), (1,)), ((), ())), preferred_element_type=jnp.float32
+            img[source, some], txt[text_window(source)], (((1,), (1,)), ((), ())),
+            preferred_element_type=jnp.float32,
         )
         inverse = jnp.exp(-BIAS_LOGIT - LOGIT_SCALE * product)
         slope = 1.0 / (1.0 + inverse)
@@ -501,7 +514,15 @@
         positive = jnp.where(diagonal, (source == z).astype(jnp.float32), 0.0)
         slope = jnp.where(positive > 0.5, -inverse * slope, slope).astype(jnp.bfloat16)
         weights[source, some] = slope
-        own_sum[source, some] = jnp.dot(slope, texts, preferred_element_type=jnp.float32)
+        return slope
+
+    def sums_of(source, start, count, slope):
+        own_sum[source, pl.ds(start, count)] = jnp.dot(
+            slope, txt[text_window(source)], preferred_element_type=jnp.float32
+        )
+
+    def weigh(source, start, count):
+        sums_of(source, start, count, slopes_of(source, start, count))
 
     def add_texts(*sources):
         slopes = jnp.concatenate([weights[source] for source in sources])
@@ -512,12 +533,21 @@
 
     def relay(target_z, sign, j):
         await_sum(target_z, sign, j)
-        arrived = sum_in[(1 - sign) // 2, target_z, piece(j)].astype(jnp.float32)
-        sum_out[target_z, piece(j)] = (own_sum[target_z, piece(j)] + arrived).astype(jnp.bfloat16)
+        arrived = sum_in[(1 - sign) // 2, target_z, part(j)].astype(jnp.float32)
+        sum_out[target_z, part(j)] = (own_sum[target_z, part(j)] + arrived).astype(jnp.bfloat16)
         sum_copy(target_z, sign, j).start()
 
     def near(j):
         relay(z + inner, inner, j)
+
+    def part_rows(slot, j):
+        return text_sum[pl.ds(pl.multiple_of(slot * rows + j * part_span, part_span), part_span)]
+
+    def part_first(j):
+        for index in (0, 1):
+            slot = 2 * index + 1
+            part_out[slot, part(j)] = part_rows(slot, j).astype(jnp.bfloat16)
+            part_to_core(index, j).start()
 
     @pl.when(is_end)
     def _():
@@ -531,7 +561,7 @@
             sum_out[source, some] = own_sum[source, some].astype(jnp.bfloat16)
 
         def give(source, low, high):
-            span_loop(low, high, lambda j: sum_copy(source, inner, j).start())
+            span_loop(2 * low, 2 * high, lambda j: sum_copy(source, inner, j).start())
 
         def far_step(j):
             take(far_z, j, 1)
@@ -541,53 +571,44 @@
         give(near_z, 0, group)
         weigh(z, 0, rows)
         add_texts(z)
+        span_loop(0, group, far_step)
+        take(edge_z, 0, group)
+        span_loop(group, pieces, far_step)
         take(near_z, group, group)
-        give(near_z, group, pieces - 1)
-        add_texts(near_z)
-        take(edge_z, 0, group)
-        loop(pieces, far_step)
-        give(near_z, pieces - 1, pieces)
-        take(edge_z, group, group)
+        give(near_z, group, pieces)
+        add_texts(far_z, near_z)
+        span_loop(group, pieces, lambda j: await_image(edge_z, j))
+        slopes_of(edge_z, group * span, group * span)
+        add_texts(edge_z)
+        loop(parts, part_first)
+        last = pl.ds(group * span, group * span)
+        sums_of(edge_z, group * span, group * span, weights[edge_z, last])
+        sum_out[edge_z, last] = own_sum[edge_z, last].astype(jnp.bfloat16)
         give(edge_z, 0, pieces)
-        add_texts(far_z, edge_z)
 
     @pl.when(is_mid)
     def _():
-        half = (ahead + pieces) // 2
-
         def image_step(index):
-            def far(j):
-                pass_image(z + 2 * inner, -inner, j)
-
             @pl.when(index == 1)
             def _():
-                span_loop(ahead, half, far)
+                span_loop(pieces + ahead, 2 * pieces - 1, pass_inner)
 
             @pl.when(index == 2)
             def _():
-                span_loop(half, pieces, far)
+                pass_inner(2 * pieces - 1)
                 span_loop(early, pieces, lambda j: image_copy(z, -inner, j).start())
-                span_loop(0, pieces // 4, near)
 
             @pl.when(index == 3)
             def _():
-                span_loop(pieces // 4, pieces // 2, near)
-
-            step = (index == 0) * 1 - (index == 1) * 1 + (index == 3) * 2
+                span_loop(0, parts // 4, near)
+
+            step = (index == 2) * 1 - (index == 0) * 1 + (index == 3) * 2
             source = z + step * inner
             weigh(source, 0, rows)
             add_texts(source)
 
         loop(4, image_step)
-
-    def part_rows(slot, j):
-        return text_sum[pl.ds(pl.multiple_of(slot * rows + j * part_span, part_span), part_span)]
-
-    def part_first(j):
-        for index in (0, 1):
-            slot = 2 * index + 1
-            part_out[slot, part(j)] = part_rows(slot, j).astype(jnp.bfloat16)
-            part_to_core(index, j).start()
+        loop(parts, part_first)
 
     def part_second(j):
         pair = part_core.at[0, pl.ds(0, 2 * part_span)]
@@ -595,15 +616,15 @@
         side = part_core[1 - core, part(j)].astype(jnp.float32)
         part_out[2, part(j)] = (part_rows(2, j) + side).astype(jnp.bfloat16)
 
-        @pl.when((odd == 1) | (j < 2 * relayed))
+        @pl.when((odd == 1) | (j < passed))
         def _():
             part_across(j).start()
 
-        @pl.when((odd == 0) & (j >= 2 * relayed))
+        @pl.when((odd == 0) & (j >= passed))
         def _():
             part_corner(j).start()
 
-        @pl.when((odd == 0) | (j >= 2 * relayed))
+        @pl.when(((odd == 0) | (j >= passed)) & ~bare)
         def _():
             part_third(j, 0.0)
 
@@ -617,33 +638,29 @@
         part_across(j).wait_recv()
         part_third(j, part_x[part(j)].astype(jnp.float32))
 
-    loop(parts, part_first)
-
-    @pl.when(is_mid)
-    def _():
-        span_loop(pieces // 2, pieces - 1, near)
-
+    def stage(i):
+        j = i - parts // 2
+
+        @pl.when(is_mid & (i < parts))
+        def _():
+            relay(z + 2 * inner, inner, i)
+
+        @pl.when(is_mid & (j >= parts // 4) & (j < parts))
+        def _():
+            near(j)
+
+        @pl.when(is_mid & (j > 0) & (j <= parts))
+        def _():
+            relay(z - inner, -inner, j - 1)
+
+        @pl.when((odd == 1) & (i >= parts - 1) & (i - parts + 1 < passed))
+        def _():
+            part_relay(i - parts + 1)
+
+    head = parts // 4 + 1
+    span_loop(0, head, stage)
     loop(parts, part_second)
-
-    @pl.when(is_mid)
-    def _():
-        loop(pieces, lambda j: relay(z + 2 * inner, inner, j))
-
-    def outer(j):
-        @pl.when((odd == 1) & (j < relayed))
-        def _():
-            part_relay(2 * j)
-            part_relay(2 * j + 1)
-
-        @pl.when(is_mid)
-        def _():
-            relay(z - inner, -inner, j)
-
-            @pl.when(j == 1)
-            def _():
-                near(pieces - 1)
-
-    loop(pieces, outer)
+    span_loop(head, 2 * parts - 1, stage)
 
     def finish(kind, out, total, j):
         wide = raw[kind, piece(j)].astype(jnp.float32)
@@ -654,27 +671,32 @@
         out[piece(j)] = ((grad - unit * radial) * scale).astype(out.dtype)
 
     def finish_text(j):
-        direct = (odd == 0) | (j >= relayed)
+        direct = (odd == 0) | (2 * j >= passed)
         for half in (0, 1):
-            part_over(2 * j + half).wait_recv()
+            @pl.when(~bare)
+            def _():
+                part_over(2 * j + half).wait_recv()
 
             @pl.when(direct)
             def _():
                 part_across(2 * j + half).wait_recv()
 
-        total = text_sum[slot_rows(0, j)] + part_y[piece(j)].astype(jnp.float32)
+        total = text_sum[slot_rows(0, j)]
+        total += jnp.where(bare, 0.0, part_y[piece(j)].astype(jnp.float32))
         total += jnp.where(core == 0, part_core[0, piece(j)].astype(jnp.float32), 0.0)
         total += jnp.where(direct, part_x[piece(j)].astype(jnp.float32), 0.0)
         finish(1, text_out, total, j)
 
     def finish_image(j):
-        await_sum(z, -inner, j)
+        for half in (0, 1):
+            await_sum(z, -inner, 2 * j + half)
+
+        @pl.when(is_mid)
+        def _():
+            for half in (0, 1):
+                await_sum(z, inner, 2 * j + half)
+
         total = own_sum[z, piece(j)] + sum_in[(1 + inner) // 2, z, piece(j)].astype(jnp.float32)
-
-        @pl.when(is_mid)
-        def _():
-            await_sum(z, inner, j)
-
         other = sum_in[(1 - inner) // 2, z, piece(j)].astype(jnp.float32)
         finish(0, image_out, total + jnp.where(is_mid, other, 0.0), j)
 
@@ -684,11 +706,20 @@
 
     loop(pieces, finish_both)
 
-    def settle(group):
-        remote(img, img, group, image_recv.at[0, 0], partner).wait_send()
-
-    for group in (0, 1, 2):
-        settle(group)
+    def settle(group, count=depth):
+        some = img.at[pl.ds(0, count)]
+        remote(some, some, group, image_recv.at[0, 0], partner).wait_send()
+
+    settle(0)
+    settle(2)
+
+    @pl.when(bare)
+    def _():
+        settle(1, 3)
+
+    @pl.when(~bare)
+    def _():
+        settle(1)
 
     @pl.when(is_mid)
     def _():
@@ -699,10 +730,10 @@
     rows, width = image_embeds.shape
     slots = window // depth + 1
     pieces = rows // PIECE_ROWS
-    early, relayed, ahead = 3 * pieces // 4, 3 * pieces // 4, pieces // 2
+    early, relayed, passed, ahead = 3 * pieces // 4, 3 * pieces // 4, 2 * pieces, pieces // 2
     low, wide = jnp.bfloat16, jnp.float32
     return pl.pallas_call(
-        functools.partial(ring_kernel, depth, window, pieces, early, relayed, ahead),
+        functools.partial(ring_kernel, depth, window, pieces, early, relayed, passed, ahead),
         out_shape=(pltpu.VMEM((rows, width), low),) * 2,
         in_specs=[pl.BlockSpec(memory_space=pl.ANY)] * 2,
         out_specs=(pl.BlockSpec(memory_space=pltpu.VMEM),) * 2,
@@ -724,7 +755,7 @@
             pltpu.SemaphoreType.DMA((depth - 1, pieces)),
             pltpu.SemaphoreType.DMA((2, pieces)),
             pltpu.SemaphoreType.DMA((2,)),
-            pltpu.SemaphoreType.DMA((depth + 1, pieces)),
+            pltpu.SemaphoreType.DMA((depth + 1, 2 * pieces)),
             pltpu.SemaphoreType.DMA((2, 2 * pieces)),
             pltpu.SemaphoreType.DMA((2 * pieces,)),
         ],

time: 41 us -> 39.5 us (0.963)
  Pallas kernels: 38.8 us -> 37 us
    pallas_call x1, Pallas kernels: 38.8 us -> 37 us  [square_call(): pl.pallas_call(functools.partial(ring_kernel, depth, window, pieces, earl...]
where the time goes in v5:
time: 39.5 us; the launch traced here: 39.1 us
  Pallas kernels  37 us (94%)
  local copies, waits for them, and re-layouts  1.43 us (4%)
  between operations  0.64 us (2%)
    pallas_call x1, Pallas kernels, square_call(): pl.pallas_call(functools.partial(ring_kernel, depth, window, pieces, earl...  37 us
    unnamed x2, local copies, waits for them, and re-layouts  1.43 us

profile of v5, /device:TPU:0, one launch (start us, length us, event | category | flops | bytes accessed | tf_op | source)
XLA Modules:
  0.0 39.1 jit_solution(5788000822156013284)
XLA Ops:
  0.6 37.0 %shard_map.41 = (bf16[128,1152]{1,0:T(8,128)(2,1)S(1)}, bf16[128,1152]{1,0:T(8,128)(2,1)S(1)}) custom-call(bf16[128,1152]{1,0:T(8,128)(2,1)} %image_ref.1, bf16[128,1152]{1,0:T(8,128)(2,1)} %text_ref.1), custom_call_target="tpu_custom_call" | custom-call | tf_op jit(solution)/shard_map/pallas_call | solution.py:735
  37.6 0.7 %copy.6 = bf16[128,1152]{1,0:T(8,128)(2,1)} copy(bf16[128,1152]{1,0:T(8,128)(2,1)S(1)} %get-tuple-element.2) | data formatting | bytes 589824
  38.3 0.7 %copy.7 = bf16[128,1152]{1,0:T(8,128)(2,1)} copy(bf16[128,1152]{1,0:T(8,128)(2,1)S(1)} %get-tuple-element.3) | data formatting | bytes 589824

commit v6 on v5

--- a/solution.py
+++ b/solution.py
@@ -256,7 +256,7 @@
     lax.fori_loop(0, depth, settle, 0)
 
 
-def ring_kernel(depth, window, pieces, early, relayed, passed, ahead, image_ref, text_ref, image_out, text_out,
+def ring_kernel(depth, window, pieces, early, relayed, passed, ahead, image_ref, text_ref, both_out,
                 raw, img, txt, own_sum, text_sum, weights, sum_out, sum_in, part_out, part_core,
                 part_x, part_y, load_sem, send, image_recv, text_recv, text_core_recv, sum_recv,
                 part_recv, part_core_recv):
@@ -588,6 +588,9 @@
 
     @pl.when(is_mid)
     def _():
+        def rest(j):
+            image_copy(z, -inner, j).start()
+
         def image_step(index):
             @pl.when(index == 1)
             def _():
@@ -596,7 +599,10 @@
             @pl.when(index == 2)
             def _():
                 pass_inner(2 * pieces - 1)
-                span_loop(early, pieces, lambda j: image_copy(z, -inner, j).start())
+
+                @pl.when(core == 0)
+                def _():
+                    span_loop(early, pieces, rest)
 
             @pl.when(index == 3)
             def _():
@@ -608,6 +614,11 @@
             add_texts(source)
 
         loop(4, image_step)
+
+        @pl.when(core == 1)
+        def _():
+            span_loop(early, pieces, rest)
+
         loop(parts, part_first)
 
     def part_second(j):
@@ -685,7 +696,7 @@
         total += jnp.where(bare, 0.0, part_y[piece(j)].astype(jnp.float32))
         total += jnp.where(core == 0, part_core[0, piece(j)].astype(jnp.float32), 0.0)
         total += jnp.where(direct, part_x[piece(j)].astype(jnp.float32), 0.0)
-        finish(1, text_out, total, j)
+        finish(1, both_out.at[pl.ds(rows, rows)], total, j)
 
     def finish_image(j):
         for half in (0, 1):
@@ -698,7 +709,7 @@
 
         total = own_sum[z, piece(j)] + sum_in[(1 + inner) // 2, z, piece(j)].astype(jnp.float32)
         other = sum_in[(1 - inner) // 2, z, piece(j)].astype(jnp.float32)
-        finish(0, image_out, total + jnp.where(is_mid, other, 0.0), j)
+        finish(0, both_out.at[pl.ds(0, rows)], total + jnp.where(is_mid, other, 0.0), j)
 
     def finish_both(j):
         finish_image(j)
@@ -732,11 +743,11 @@
     pieces = rows // PIECE_ROWS
     early, relayed, passed, ahead = 3 * pieces // 4, 3 * pieces // 4, 2 * pieces, pieces // 2
     low, wide = jnp.bfloat16, jnp.float32
-    return pl.pallas_call(
+    both = pl.pallas_call(
         functools.partial(ring_kernel, depth, window, pieces, early, relayed, passed, ahead),
-        out_shape=(pltpu.VMEM((rows, width), low),) * 2,
+        out_shape=pltpu.VMEM((2 * rows, width), low),
         in_specs=[pl.BlockSpec(memory_space=pl.ANY)] * 2,
-        out_specs=(pl.BlockSpec(memory_space=pltpu.VMEM),) * 2,
+        out_specs=pl.BlockSpec(memory_space=pltpu.VMEM),
         scratch_shapes=[
             pltpu.VMEM((2, rows, width), low),
             pltpu.VMEM((depth, rows, width), low),
@@ -761,6 +772,7 @@
         ],
         compiler_params=pltpu.CompilerParams(collective_id=0, has_side_effects=True),
     )(image_embeds, text_embeds)
+    return both[:rows], both[rows:]
 
 
 def solution(mesh):

time: 39.5 us -> 38.7 us (0.980)
  local copies, waits for them, and re-layouts: 1.43 us -> 0.86 us
    unnamed x2 -> x0, local copies, waits for them, and re-layouts: 1.43 us -> none
    slice x0 -> x1, local copies, waits for them, and re-layouts: none -> 0.86 us  [square_call(): return (both[:rows], both[rows:])]
where the time goes in v6:
time: 38.7 us; the launch traced here: 38.5 us
  Pallas kernels  37 us (96%)
  local copies, waits for them, and re-layouts  0.86 us (2%)
  between operations  0.64 us (2%)
    pallas_call x1, Pallas kernels, square_call(): pl.pallas_call(functools.partial(ring_kernel, depth, window, pieces, earl...  37 us
    slice x1, local copies, waits for them, and re-layouts, square_call(): return (both[:rows], both[rows:])  0.86 us

profile of v6, /device:TPU:0, one launch (start us, length us, event | category | flops | bytes accessed | tf_op | source)
XLA Modules:
  0.0 38.5 jit_solution(15579126804877697402)
XLA Ops:
  0.6 37.0 %shard_map.41 = bf16[256,1152]{1,0:T(8,128)(2,1)S(1)} custom-call(bf16[128,1152]{1,0:T(8,128)(2,1)} %image_ref.1, bf16[128,1152]{1,0:T(8,128)(2,1)} %text_ref.1), custom_call_target="tpu_custom_call" | custom-call | tf_op jit(solution)/shard_map/pallas_call | solution.py:746
  37.6 0.9 %fusion = (bf16[128,1152]{1,0:T(8,128)(2,1)}, bf16[128,1152]{1,0:T(8,128)(2,1)}) fusion(bf16[256,1152]{1,0:T(8,128)(2,1)S(1)} %shard_map.41), kind=kLoop, calls=%fused_computation | loop fusion | bytes 1179648 | tf_op jit(solution)/shard_map/slice | solution.py:775

commit v7 on v6

--- a/solution.py
+++ b/solution.py
@@ -490,6 +490,12 @@
             second(j - ahead)
 
     loop(pieces + ahead, first)
+    waiting = (odd == 0) & (core == 1)
+
+    @pl.when(is_mid & waiting)
+    def _():
+        span_loop(pieces + ahead, 2 * pieces - 1, pass_inner)
+
     for index in (0, 1):
         slot = 2 * index + 1
         block = txt.at[pl.ds(slot * rows, rows)]
@@ -592,7 +598,7 @@
             image_copy(z, -inner, j).start()
 
         def image_step(index):
-            @pl.when(index == 1)
+            @pl.when((index == 1) & ~waiting)
             def _():
                 span_loop(pieces + ahead, 2 * pieces - 1, pass_inner)
 
@@ -631,7 +637,7 @@
         def _():
             part_across(j).start()
 
-        @pl.when((odd == 0) & (j >= passed))
+        @pl.when((odd == 0) & (j >= passed) & (~bare | (j < parts // 2)))
         def _():
             part_corner(j).start()
 
@@ -650,7 +656,7 @@
         part_third(j, part_x[part(j)].astype(jnp.float32))
 
     def stage(i):
-        j = i - parts // 2
+        j = i - parts // 2 - 1
 
         @pl.when(is_mid & (i < parts))
         def _():
@@ -668,7 +674,7 @@
         def _():
             part_relay(i - parts + 1)
 
-    head = parts // 4 + 1
+    head = parts // 2
     span_loop(0, head, stage)
     loop(parts, part_second)
     span_loop(head, 2 * parts - 1, stage)
@@ -713,6 +719,11 @@
 
     def finish_both(j):
         finish_image(j)
+
+        @pl.when(bare & (odd == 0) & (j == 0))
+        def _():
+            span_loop(parts // 2, parts, lambda i: part_corner(i).start())
+
         finish_text(j)
 
     loop(pieces, finish_both)

time: 38.7 us -> 38.7 us (level)
  no operation moved by 1% of the time
where the time goes in v7:
time: 38.7 us; the launch traced here: 38.4 us
  Pallas kernels  36.9 us (95%)
  local copies, waits for them, and re-layouts  0.86 us (2%)
  between operations  0.64 us (2%)
    pallas_call x1, Pallas kernels, square_call(): pl.pallas_call(functools.partial(ring_kernel, depth, window, pieces, earl...  36.9 us
    slice x1, local copies, waits for them, and re-layouts, square_call(): return (both[:rows], both[rows:])  0.86 us

profile of v7, /device:TPU:0, one launch (start us, length us, event | category | flops | bytes accessed | tf_op | source)
XLA Modules:
  0.0 38.4 jit_solution(9246144949992977627)
XLA Ops:
  0.6 36.9 %shard_map.41 = bf16[256,1152]{1,0:T(8,128)(2,1)S(1)} custom-call(bf16[128,1152]{1,0:T(8,128)(2,1)} %image_ref.1, bf16[128,1152]{1,0:T(8,128)(2,1)} %text_ref.1), custom_call_target="tpu_custom_call" | custom-call | tf_op jit(solution)/shard_map/pallas_call | solution.py:757
  37.6 0.9 %fusion = (bf16[128,1152]{1,0:T(8,128)(2,1)}, bf16[128,1152]{1,0:T(8,128)(2,1)}) fusion(bf16[256,1152]{1,0:T(8,128)(2,1)S(1)} %shard_map.41), kind=kLoop, calls=%fused_computation | loop fusion | bytes 1179648 | tf_op jit(solution)/shard_map/slice | solution.py:786

commit v8 on v7

--- a/solution.py
+++ b/solution.py
@@ -314,22 +314,26 @@
         await_image(source_z, j)
         image_copy(source_z, sign, j).start()
 
-    def sum_slot(target_z, there, sign):
+    def sum_slot(target_z, there, sign, j):
         distance = target_z - there
         distance = jnp.maximum(distance, -distance)
-        return jnp.where(sign == 1 - 2 * (there // 2), distance, depth - 1 + distance)
+        inward = sign == 1 - 2 * (there // 2)
+        own = distance == 0
+        row = jnp.where(own, 0, jnp.where(inward, distance, depth - 1))
+        column = jnp.where(own, j // 2 + jnp.where(inward, 0, pieces), j)
+        return sum_recv.at[row, column]
 
     def sum_copy(target_z, sign, j):
         there = along(sign)
         return remote(
             sum_out.at[target_z, part(j)], sum_in.at[(1 - sign) // 2, target_z, part(j)], 2,
-            sum_recv.at[sum_slot(target_z, there[1], sign), j], there,
+            sum_slot(target_z, there[1], sign, j), there,
         )
 
     def await_sum(target_z, sign, j):
         remote(
             sum_out.at[target_z, part(j)], sum_in.at[(1 - sign) // 2, target_z, part(j)], 2,
-            sum_recv.at[sum_slot(target_z, z, sign), j], along(inner),
+            sum_slot(target_z, z, sign, j), along(inner),
         ).wait_recv()
 
     def text_copy(source_slot, target_slot, recv, j, device):
@@ -358,17 +362,17 @@
 
     def part_across(j):
         return remote(
-            part_out.at[2, part(j)], part_x.at[part(j)], 1, part_recv.at[0, j], across
+            part_out.at[2, part(j)], part_x.at[part(j)], 1, part_recv.at[j // pieces, j % pieces], across
         )
 
     def part_corner(j):
         return remote(
-            part_out.at[2, part(j)], part_x.at[part(j)], 1, part_recv.at[0, j], corner
+            part_out.at[2, part(j)], part_x.at[part(j)], 1, part_recv.at[j // pieces, j % pieces], corner
         )
 
     def part_over(j):
         return remote(
-            part_out.at[4, part(j)], part_y.at[part(j)], 1, part_recv.at[1, j], over
+            part_out.at[4, part(j)], part_y.at[part(j)], 1, part_recv.at[2, j // 2], over
         )
 
     def span_loop(low, high, body):
@@ -689,13 +693,15 @@
 
     def finish_text(j):
         direct = (odd == 0) | (2 * j >= passed)
-        for half in (0, 1):
-            @pl.when(~bare)
-            def _():
-                part_over(2 * j + half).wait_recv()
-
-            @pl.when(direct)
-            def _():
+        @pl.when(~bare)
+        def _():
+            remote(
+                part_out.at[4, piece(j)], part_y.at[piece(j)], 1, part_recv.at[2, j], over
+            ).wait_recv()
+
+        @pl.when(direct)
+        def _():
+            for half in (0, 1):
                 part_across(2 * j + half).wait_recv()
 
         total = text_sum[slot_rows(0, j)]
@@ -704,14 +710,18 @@
         total += jnp.where(direct, part_x[piece(j)].astype(jnp.float32), 0.0)
         finish(1, both_out.at[pl.ds(rows, rows)], total, j)
 
+    def await_own(sign, j):
+        remote(
+            sum_out.at[z, piece(j)], sum_in.at[(1 - sign) // 2, z, piece(j)], 2,
+            sum_slot(z, z, sign, 2 * j), along(inner),
+        ).wait_recv()
+
     def finish_image(j):
-        for half in (0, 1):
-            await_sum(z, -inner, 2 * j + half)
+        await_own(-inner, j)
 
         @pl.when(is_mid)
         def _():
-            for half in (0, 1):
-                await_sum(z, inner, 2 * j + half)
+            await_own(inner, j)
 
         total = own_sum[z, piece(j)] + sum_in[(1 + inner) // 2, z, piece(j)].astype(jnp.float32)
         other = sum_in[(1 - inner) // 2, z, piece(j)].astype(jnp.float32)
@@ -777,8 +787,8 @@
             pltpu.SemaphoreType.DMA((depth - 1, pieces)),
             pltpu.SemaphoreType.DMA((2, pieces)),
             pltpu.SemaphoreType.DMA((2,)),
-            pltpu.SemaphoreType.DMA((depth + 1, 2 * pieces)),
-            pltpu.SemaphoreType.DMA((2, 2 * pieces)),
+            pltpu.SemaphoreType.DMA((depth, 2 * pieces)),
+            pltpu.SemaphoreType.DMA((3, pieces)),
             pltpu.SemaphoreType.DMA((2 * pieces,)),
         ],
         compiler_params=pltpu.CompilerParams(collective_id=0, has_side_effects=True),

time: 38.7 us -> 38.6 us (level)
  no operation moved by 1% of the time
where the time goes in v8:
time: 38.6 us; the launch traced here: 38.3 us
  Pallas kernels  36.8 us (95%)
  local copies, waits for them, and re-layouts  0.86 us (2%)
  between operations  0.64 us (2%)
    pallas_call x1, Pallas kernels, square_call(): pl.pallas_call(functools.partial(ring_kernel, depth, window, pieces, earl...  36.8 us
    slice x1, local copies, waits for them, and re-layouts, square_call(): return (both[:rows], both[rows:])  0.86 us

profile of v8, /device:TPU:0, one launch (start us, length us, event | category | flops | bytes accessed | tf_op | source)
XLA Modules:
  0.0 38.3 jit_solution(1764965315626877332)
XLA Ops:
  0.6 36.8 %shard_map.41 = bf16[256,1152]{1,0:T(8,128)(2,1)S(1)} custom-call(bf16[128,1152]{1,0:T(8,128)(2,1)} %image_ref.1, bf16[128,1152]{1,0:T(8,128)(2,1)} %text_ref.1), custom_call_target="tpu_custom_call" | custom-call | tf_op jit(solution)/shard_map/pallas_call | solution.py:767
  37.5 0.9 %fusion = (bf16[128,1152]{1,0:T(8,128)(2,1)}, bf16[128,1152]{1,0:T(8,128)(2,1)}) fusion(bf16[256,1152]{1,0:T(8,128)(2,1)S(1)} %shard_map.41), kind=kLoop, calls=%fused_computation | loop fusion | bytes 1179648 | tf_op jit(solution)/shard_map/slice | solution.py:796
